TPU v7x, 8 devices: a whole 2x2x1 slice. The times are simulated.
8 devices in a mesh: rep: 2 (over y, z), dp: 4 (over x, core).
Axes of the slice: x: 2, y: 2, z: 1, core: 2. Of those that a mesh axis runs over, the one named last changes fastest.
Arguments:
- x: bfloat16 [8, 2048, 1536], P(('rep', 'dp')), parts along dimension 0
- dy: bfloat16 [8, 2048, 1536], P(('rep', 'dp')), parts along dimension 0
- w_gate: bfloat16 [2, 1536, 3584], replicated
- w_up: bfloat16 [2, 1536, 3584], replicated
- w_down: bfloat16 [2, 3584, 1536], replicated
- m_w_gate: float32 [2, 1536, 3584], replicated
- m_w_up: float32 [2, 1536, 3584], replicated
- m_w_down: float32 [2, 3584, 1536], replicated
- v_w_gate: float32 [2, 1536, 3584], replicated
- v_w_up: float32 [2, 1536, 3584], replicated
- v_w_down: float32 [2, 3584, 1536], replicated
Outputs:
- output 1: bfloat16 [4, 1536, 3584], P('rep'), parts along dimension 0
- output 2: bfloat16 [4, 1536, 3584], P('rep'), parts along dimension 0
- output 3: bfloat16 [4, 3584, 1536], P('rep'), parts along dimension 0
- output 4: float32 [4, 1536, 3584], P('rep'), parts along dimension 0
- output 5: float32 [4, 1536, 3584], P('rep'), parts along dimension 0
- output 6: float32 [4, 3584, 1536], P('rep'), parts along dimension 0
- output 7: float32 [4, 1536, 3584], P('rep'), parts along dimension 0
- output 8: float32 [4, 1536, 3584], P('rep'), parts along dimension 0
- output 9: float32 [4, 3584, 1536], P('rep'), parts along dimension 0
There are 2 independent parts. A program takes and returns all parts, laid end to end along the dimension named above; an argument that names none is the same for every part.
All inputs are finite; a program needn't handle non-finite values.
Results may differ from a plain program's by a relative error of at most 0.02.
Values are sent between devices in bfloat16 or wider.
A program may use at most 3 GiB of HBM per device.

v0:
```python
import jax
import jax.numpy as jnp
from jax import lax
from jax.sharding import PartitionSpec as P

NAMES = ("w_gate", "w_up", "w_down")


def matmul(a, w):
    return jnp.dot(a, w, preferred_element_type=jnp.float32).astype(jnp.bfloat16)


def normed(h):
    wide = h.astype(jnp.float32)
    scale = lax.rsqrt(jnp.mean(wide**2, -1, keepdims=True) + 1e-6)
    return (wide * scale).astype(jnp.bfloat16)


def layer(h, w):
    a = normed(h)
    gate = jnp.dot(a, w["w_gate"], preferred_element_type=jnp.float32)
    up = jnp.dot(a, w["w_up"], preferred_element_type=jnp.float32)
    return h + matmul((jax.nn.silu(gate) * up).astype(jnp.bfloat16), w["w_down"])


def adamw(w, m, v, g):
    m = 0.9 * m + 0.1 * g
    v = 0.95 * v + 0.05 * g * g
    step = m * lax.rsqrt(v + 1e-8) + 0.1 * w
    return (w - 0.02 * step).astype(jnp.bfloat16), m, v


def solution(mesh):
    def step(x, dy, *arrays):
        weights, m, v = (arrays[i : i + 3] for i in (0, 3, 6))
        layers = weights[0].shape[0]
        h, kept = x[0], []
        for number in range(layers):
            kept.append(h)
            h = layer(h, {name: w[number] for name, w in zip(NAMES, weights, strict=True)})
        by_h, summed = dy[0], [None] * layers
        for number in reversed(range(layers)):
            _, back = jax.vjp(lambda w, h: layer(h, w), {name: w[number] for name, w in zip(NAMES, weights, strict=True)}, kept[number])
            by_w, by_h = back(by_h)
            summed[number] = [lax.psum(by_w[name], "dp") for name in NAMES]
        gradients = [jnp.stack([summed[number][i] for number in range(layers)]).astype(jnp.float32) for i in range(3)]
        new = [adamw(w.astype(jnp.float32), m, v, g) for w, m, v, g in zip(weights, m, v, gradients, strict=True)]
        return tuple(one[which] for which in range(3) for one in new)

    return jax.shard_map(
        step,
        mesh=mesh,
        in_specs=(P(("rep", "dp"), None, None),) * 2 + (P(None, None, None),) * 9,
        out_specs=(P("rep", None, None),) * 9,
        check_vma=False,
    )
```

profile of v0, /device:TPU:0, one launch (start us, length us, event | category | flops | bytes accessed | tf_op | source)
XLA Modules:
  0.0 1875.6 jit_solution(13860995009521758742)
XLA Ops:
  7.2 0.0 all-reduce.3.cloned.1.call-start
  7.2 8.6 copy.20
  15.8 4.1 fusion.42
  20.0 0.0 copy-start.2
  20.0 31.7 %fusion.62 = f32[2048,3584]{1,0:T(8,128)} fusion(bf16[2,1536,3584]{2,1,0:T(8,128)(2,1)} %param.13, bf16[1,2048,1536]{2,1,0:T(8,128)(2,1)} %param.11, f32[2048]{0:T(1024)S(1)} %add_rsqrt_fusion), kind=kOutput, calls=%fused_computation.95 | convolution fusion | flops 22558015488 | bytes 46669824 | tf_op jit(solution)/shard_map/dot_general | solution.py:21
  51.7 0.0 copy-done.2
  51.7 40.3 %multiply_convert_fusion.1 = (bf16[2048,3584]{1,0:T(8,128)(2,1)}, f32[2048,3584]{1,0:T(8,128)}) fusion(f32[2048,3584]{1,0:T(8,128)} %fusion.62, bf16[2,1536,3584]{2,1,0:T(8,128)(2,1)} %param.14, bf16[1,2048,1536]{2,1,0:T(8,128)(2,1)} %param.11, f32[2048]{0:T(1024)S(1)} %add_rsqrt_fusion), kind=kOutput, calls=%fused_computation.44 | convolution fusion | flops 22602055680 | bytes 90710016 | tf_op jit(solution)/shard_map/dot_general | solution.py:22
  92.0 32.0 %fusion.46 = (f32[2048]{0:T(1024)S(1)}, bf16[2048,1536]{0,1:T(8,128)(2,1)}) fusion(bf16[2048,3584]{1,0:T(8,128)(2,1)} %get-tuple-element.24, bf16[2,3584,1536]{2,1,0:T(8,128)(2,1)} %param.15, bf16[1,2048,1536]{1,2,0:T(8,128)(2,1)} %copy.20), kind=kOutput, calls=%fused_computation.78 | convolution fusion | flops 22564304896 | bytes 38281216 | tf_op jit(solution)/shard_map/dot_general | solution.py:10
  124.0 0.0 copy-start
  124.0 30.0 %convolution_convert_fusion.4 = bf16[2048,3584]{1,0:T(8,128)(2,1)} fusion(bf16[2,3584,1536]{2,1,0:T(8,128)(2,1)} %param.15, bf16[1,2048,1536]{2,1,0:T(8,128)(2,1)} %param.12), kind=kOutput, calls=%fused_computation.66 | convolution fusion | flops 22555918336 | bytes 31981568 | tf_op jit(solution)/shard_map/transpose(jvp())/dot_general | solution.py:10
  154.0 0.0 copy-done
  154.0 31.9 %fusion.49 = f32[2048,3584]{1,0:T(8,128)} fusion(bf16[2,1536,3584]{2,1,0:T(8,128)(2,1)} %param.14, bf16[2048,1536]{0,1:T(8,128)(2,1)} %get-tuple-element.27, f32[2048]{0:T(1024)S(1)} %fusion.100), kind=kOutput, calls=%fused_computation.82 | convolution fusion | flops 22558015488 | bytes 46669824 | tf_op jit(solution)/shard_map/jvp()/dot_general | solution.py:22
  185.9 45.3 %fusion.17 = (bf16[2048,3584]{1,0:T(8,128)(2,1)}, f32[2048,3584]{1,0:T(8,128)}) fusion(f32[2048,3584]{1,0:T(8,128)} %fusion.49, bf16[2048,3584]{1,0:T(8,128)(2,1)} %convolution_convert_fusion.4, bf16[2,1536,3584]{2,1,0:T(8,128)(2,1)} %param.13, bf16[2048,1536]{0,1:T(8,128)(2,1)} %get-tuple-element.27, f32[2048]{0:T(1024)S(1)} %fusion.100), kind=kOutput, calls=%fused_computation.35 | convolution fusion | flops 22646095872 | bytes 105390080 | tf_op jit(solution)/shard_map/jvp()/dot_general | solution.py:21
  231.2 30.4 %fusion.37 = bf16[1,1536,3584]{2,1,0:T(8,128)(2,1)} fusion(bf16[2048,3584]{1,0:T(8,128)(2,1)} %get-tuple-element.28, bf16[2048,1536]{0,1:T(8,128)(2,1)} %get-tuple-element.27, f32[2048]{0:T(1024)S(1)} %fusion.100), kind=kOutput, calls=%fused_computation.71 | convolution fusion | flops 22558015488 | bytes 31989760 | tf_op jit(solution)/shard_map/transpose(jvp())/dot_general | solution.py:21
  261.6 30.4 %fusion.76 = bf16[2048,1536]{0,1:T(8,128)(2,1)} fusion(bf16[2048,3584]{1,0:T(8,128)(2,1)} %get-tuple-element.28, bf16[2,1536,3584]{2,1,0:T(8,128)(2,1)} %param.13), kind=kOutput, calls=%fused_computation.107 | convolution fusion | flops 22548578304 | bytes 31981568 | tf_op jit(solution)/shard_map/transpose(jvp())/dot_general | solution.py:21
  292.0 8.6 copy.21
  300.6 35.1 %fusion.36 = bf16[1,1536,3584]{2,1,0:T(8,128)(2,1)} fusion(bf16[2048,3584]{1,0:T(8,128)(2,1)} %convolution_convert_fusion.4, bf16[2048,1536]{0,1:T(8,128)(2,1)} %get-tuple-element.27, f32[2048]{0:T(1024)S(1)} %fusion.100, f32[2048,3584]{1,0:T(8,128)} %get-tuple-element.29), kind=kOutput, calls=%fused_computation.70 | convolution fusion | flops 22607560704 | bytes 61349888 | tf_op jit(solution)/shard_map/transpose(jvp())/dot_general | solution.py:22
  335.7 33.7 %fusion.34 = bf16[1,3584,1536]{2,1,0:T(8,128)(2,1)} fusion(f32[2048,3584]{1,0:T(8,128)} %fusion.49, bf16[1,2048,1536]{2,1,0:T(8,128)(2,1)} %param.12, f32[2048,3584]{1,0:T(8,128)} %get-tuple-element.29), kind=kOutput, calls=%fused_computation.68 | convolution fusion | flops 22598123520 | bytes 76021760 | tf_op jit(solution)/shard_map/transpose(jvp())/dot_general | solution.py:10
  369.4 0.0 copy-start.1
  369.4 45.1 %fusion.48 = (f32[2048]{0:T(1024)S(1)}, bf16[2048,1536]{0,1:T(8,128)(2,1)}) fusion(bf16[2048,1536]{0,1:T(8,128)(2,1)} %get-tuple-element.27, bf16[2048,1536]{0,1:T(8,128)(2,1)} %fusion.76, bf16[2,1536,3584]{2,1,0:T(8,128)(2,1)} %param.14, bf16[2048,3584]{1,0:T(8,128)(2,1)} %convolution_convert_fusion.4, f32[2048,3584]{1,0:T(8,128)} %get-tuple-element.29), kind=kOutput, calls=%fused_computation.80 | convolution fusion | flops 22611490816 | bytes 73932800 | tf_op jit(solution)/shard_map/transpose(jvp())/dot_general | solution.py:22
  414.5 0.0 copy-done.1
  414.5 11.7 fusion.83
  426.2 0.0 slice-start
  426.2 30.4 %convolution_convert_fusion.3 = bf16[2048,3584]{1,0:T(8,128)(2,1)} fusion(bf16[2048,1536]{0,1:T(8,128)(2,1)} %fusion.83, bf16[2,3584,1536]{2,1,0:T(8,128)(2,1)} %param.15), kind=kOutput, calls=%fused_computation.65 | convolution fusion | flops 22555918336 | bytes 31981568 | tf_op jit(solution)/shard_map/transpose(jvp())/dot_general | solution.py:10
  456.6 0.0 slice-start.1
  456.7 0.0 copy-start.3
  456.7 29.4 %fusion.38 = bf16[1,3584,1536]{2,1,0:T(8,128)(2,1)} fusion(bf16[2048,3584]{1,0:T(8,128)(2,1)} %get-tuple-element.24, bf16[2048,1536]{0,1:T(8,128)(2,1)} %fusion.83), kind=kOutput, calls=%fused_computation.72 | convolution fusion | flops 22554083328 | bytes 31981568 | tf_op jit(solution)/shard_map/transpose(jvp())/dot_general | solution.py:10
  486.1 0.0 slice-done
  486.1 0.0 slice-done.1
  486.1 0.0 copy-done.3
  486.1 33.6 %fusion.35 = bf16[1,1536,3584]{2,1,0:T(8,128)(2,1)} fusion(bf16[2048,3584]{1,0:T(8,128)(2,1)} %convolution_convert_fusion.3, bf16[1,2048,1536]{1,2,0:T(8,128)(2,1)S(1)} %bitcast.81, f32[2048]{0:T(1024)S(1)} %copy-done.3, f32[2048,3584]{1,0:T(8,128)} %fusion.62), kind=kOutput, calls=%fused_computation.69 | convolution fusion | flops 22607560704 | bytes 61349888 | tf_op jit(solution)/shard_map/transpose(jvp())/dot_general | solution.py:22
  519.6 39.3 %fusion.39 = bf16[1,1536,3584]{2,1,0:T(8,128)(2,1)} fusion(f32[2048,3584]{1,0:T(8,128)} %fusion.62, f32[2048,3584]{1,0:T(8,128)} %get-tuple-element.25, bf16[2048,3584]{1,0:T(8,128)(2,1)} %convolution_convert_fusion.3, bf16[1,2048,1536]{1,2,0:T(8,128)(2,1)} %copy.20, f32[2048]{0:T(1024)S(1)} %copy-done.3), kind=kOutput, calls=%fused_computation.73 | convolution fusion | flops 22644260864 | bytes 90710016 | tf_op jit(solution)/shard_map/transpose(jvp())/dot_general | solution.py:21
  559.0 0.0 all-reduce.3.cloned.1.call-update
  559.0 1077.6 %all-reduce.3.cloned.1.call-done = (bf16[1,1536,3584]{2,1,0:T(8,128)(2,1)}, bf16[1,1536,3584]{2,1,0:T(8,128)(2,1)}, bf16[1,1536,3584]{2,1,0:T(8,128)(2,1)}, bf16...) async-done(((bf16[1,1536,3584]{2,1,0:T(8,128)(2,1)}, bf16[1,1536,3584]{2,1,0:T(8,128)(2,1)}, ...) | async-done | bytes 66060304 | tf_op jit(solution)/shard_map/psum | solution.py:45
  1636.6 79.8 %fusion.10 = (bf16[2,3584,1536]{2,1,0:T(8,128)(2,1)}, f32[2,3584,1536]{2,1,0:T(8,128)}, f32[2,3584,1536]{2,1,0:T(8,128)}) fusion(bf16[2,3584,1536]{2,1,0:T(8,128)(2,1)} %param.15, bf16[1,3584,1536]{2,1,0:T(8,128)(2,1)} %get-tuple-element.13, bf16[1,3584,1536]{2,1,0:T(8,128)(2,1)} %get-tuple-element.14, f32[2,3584,1536]{2,1,0:T(8,128)} %param.21, ...), kind=kLoop, calls=%fused_computation.22 | loop fusion | flops 209190912 | bytes 242221056 | tf_op jit(solution)/shard_map/convert_element_type | solution.py:30
  1716.4 152.0 %fusion.2 = (bf16[2,1536,3584]{2,1,0:T(8,128)(2,1)}, f32[2,1536,3584]{2,1,0:T(8,128)}, f32[2,1536,3584]{2,1,0:T(8,128)}, bf16[2,1536,3584]{2,1,0:T(8,128)(2,1)},...) fusion(bf16[2,1536,3584]{2,1,0:T(8,128)(2,1)} %param.13, bf16[1,1536,3584]{2,1,0:T(8,128)(2,1)} %get-tuple-element.9, ...), kind=kLoop, calls=%fused_computation.14 | loop fusion | flops 418381824 | bytes 484442112 | tf_op jit(solution)/shard_map/convert_element_type | solution.py:30
  (4 shorter events, 0.0 us)
Async XLA Ops:
  7.2 1629.4 %all-reduce.3.cloned.1.call-start = ((), (), s32[]{:S(2)}) async-start(), calls=%async_computation | async-start | bytes 132120576 | tf_op jit(solution)/shard_map/psum | solution.py:45
  20.0 31.8 %copy-start.2 = (f32[2048]{0:T(1024)}, f32[2048]{0:T(1024)S(1)}, u32[]{:S(2)}) copy-start(f32[2048]{0:T(1024)S(1)} %add_rsqrt_fusion) | copy-start | bytes 24580
  124.0 30.0 %copy-start = (f32[2048]{0:T(1024)}, f32[2048]{0:T(1024)S(1)}, u32[]{:S(2)}) copy-start(f32[2048]{0:T(1024)S(1)} %get-tuple-element.26) | copy-start | bytes 24580
  369.4 45.1 %copy-start.1 = (f32[2048]{0:T(1024)S(1)}, f32[2048]{0:T(1024)}, u32[]{:S(2)}) copy-start(f32[2048]{0:T(1024)} %copy-done) | copy-start | bytes 24580
  426.2 59.9 %slice-start = ((s8[6291456]{0:T(1024)(128)(4,1)}), s8[2097152]{0:T(1024)(128)(4,1)S(1)}, s32[]{:S(2)}) async-start(s8[6291456]{0:T(1024)(128)(4,1)} %bitcast.80), calls=%async_computation.1 | async-start | bytes 4194304
  456.6 29.4 %slice-start.1 = ((s8[6291456]{0:T(1024)(128)(4,1)}), s8[4194304]{0:T(1024)(128)(4,1)S(1)}, s32[]{:S(2)}) async-start(s8[6291456]{0:T(1024)(128)(4,1)} %bitcast.80), calls=%async_computation.2 | async-start | bytes 8388608
  456.7 29.4 %copy-start.3 = (f32[2048]{0:T(1024)S(1)}, f32[2048]{0:T(1024)}, u32[]{:S(2)}) copy-start(f32[2048]{0:T(1024)} %copy-done.2) | copy-start | bytes 24580
Sparse Core Ops, SparseCore 0:
  559.1 1077.4 all-reduce.2
where the time goes:
time: 1890 us; the launch traced here: 1880 us
  waiting for transfers between devices  1080 us (57%)
  matrix products  519 us (27%)
  other arithmetic  248 us (13%)
    psum x1, waiting for transfers between devices, step(): summed[number] = [lax.psum(by_w[name], 'dp') for name in NAMES]  1080 us
    convert_element_type x2, other arithmetic, adamw(): return ((w - 0.02 * step).astype(jnp.bfloat16), m, v)  232 us
    dot_general x5, matrix products, layer(): up = jnp.dot(a, w['w_up'], preferred_element_type=jnp.float32)  186 us
    dot_general x5, matrix products, layer(): gate = jnp.dot(a, w['w_gate'], preferred_element_type=jnp.float32)  177 us
    dot_general x5, matrix products, matmul(): jnp.dot(a, w, preferred_element_type=jnp.float32).astype(jnp.bfloat16)  156 us
  transfers between devices with their start and end apart: 1, of which 1 were waited for; matrix products, arithmetic and copies ran while one was open for 0% of the time, Pallas kernels for 0%

commit v1 on v0

v1 whole, which is shorter than its diff:
```python
import jax
import jax.numpy as jnp
from jax import lax
from jax.experimental import pallas as pl
from jax.experimental.pallas import tpu as pltpu
from jax.sharding import PartitionSpec as P


F32, BF16 = jnp.float32, jnp.bfloat16
PARTNER = [(0, 1), (1, 0), (2, 3), (3, 2)]
ACROSS = [(0, 2), (2, 0), (1, 3), (3, 1)]


def dot(a, b, dims):
    return lax.dot_general(a, b, (dims, ((), ())), preferred_element_type=F32)


def scale_of(h):
    wide = h.astype(F32)
    return lax.rsqrt(jnp.mean(wide**2, -1, keepdims=True) + 1e-6)


def normed(h):
    return (h.astype(F32) * scale_of(h)).astype(BF16)


def adamw_kernel(side, g, w, m, v, *refs):
    new_w, new_m, new_v = refs[-3:]
    g = g[...].astype(F32)[None]
    one = 0.9 * m[...] + 0.1 * g
    two = 0.95 * v[...] + 0.05 * g * g
    step = one * lax.rsqrt(two + 1e-8) + 0.1 * w[...].astype(F32)
    new_w[...] = (w[...].astype(F32) - 0.02 * step).astype(BF16)
    new_m[...] = one
    new_v[...] = two


def adamw(side, g, w, m, v, layer, by_rows, so_far):
    rows, cols = g.shape
    tile = 96 if by_rows else 256
    steps = rows // tile
    if by_rows:
        where = lambda i, s: (layer, s[0] * steps + i, 0)
    else:
        where = lambda i, s: (layer, i, s[0])
    block = pl.BlockSpec((1, tile, cols), where)
    kept = [] if so_far is None else list(so_far)
    return pl.pallas_call(
        adamw_kernel,
        grid_spec=pltpu.PrefetchScalarGridSpec(
            num_scalar_prefetch=1,
            grid=(steps,),
            in_specs=[pl.BlockSpec((tile, cols), lambda i, s: (i, 0)), block, block, block] + [pl.BlockSpec(memory_space=pl.ANY)] * len(kept),
            out_specs=[block] * 3,
        ),
        out_shape=[jax.ShapeDtypeStruct(w.shape, BF16), jax.ShapeDtypeStruct(w.shape, F32), jax.ShapeDtypeStruct(w.shape, F32)],
        input_output_aliases={5 + i: i for i in range(len(kept))},
        cost_estimate=pl.CostEstimate(flops=rows * cols * 4000, bytes_accessed=rows * cols * 22, transcendentals=rows * cols),
        name="adamw",
    )(side, g, w, m, v, *kept)


def solution(mesh):
    def step(x, dy, *arrays):
        weights, m, v = (arrays[i : i + 3] for i in (0, 3, 6))
        layers = weights[0].shape[0]
        h, dy = x[0], dy[0]
        half = h.shape[-1] // 2
        me = lax.axis_index("dp") % 2
        mine, others = me.astype(jnp.int32)[None], (1 - me).astype(jnp.int32)[None]
        w_gate, w_up, w_down = ([w[n] for n in range(layers)] for w in weights)
        kept = []
        for n in range(layers):
            a = normed(h)
            gate, up = (dot(a, w[n], ((1,), (0,))) for w in (w_gate, w_up))
            hidden = (jax.nn.silu(gate) * up).astype(BF16)
            kept.append((h, a, gate, up, hidden))
            if n < layers - 1:
                h = h + dot(hidden, w_down[n], ((1,), (0,))).astype(BF16)

        def after(x, *others):
            return lax.optimization_barrier((x, *others))[0]

        waiting = []

        def reduce(which, layer, thin, wide):
            by_rows = which < 2

            def term(piece):
                return (dot(piece, wide, ((0,), (0,))) if by_rows else dot(wide, piece, ((0,), (0,)))).astype(BF16)

            theirs, ours = (lax.dynamic_slice(thin, (0, side * half), (thin.shape[0], half)) for side in (1 - me, me))
            first = lax.optimization_barrier(term(theirs))
            got = lax.ppermute(first, "dp", PARTNER)
            second = term(after(ours, first))
            own = lax.optimization_barrier((second.astype(F32) + got.astype(F32)).astype(BF16))
            far = lax.ppermute(own, "dp", ACROSS)
            waiting.append((which, layer, own, far))
            return own

        by = dy
        for n in reversed(range(layers)):
            h, a, gate, up, hidden = kept[n]
            done = reduce(2, n, by, hidden)
            by_hidden = dot(after(by, done), w_down[n], ((1,), (1,))).astype(BF16).astype(F32)
            sig = jax.nn.sigmoid(gate)
            by_up = (by_hidden * (gate * sig)).astype(BF16)
            by_gate = (by_hidden * up * (sig * (1 + gate * (1 - sig)))).astype(BF16)
            a, by_up, by_gate = lax.optimization_barrier((a, by_up, by_gate))
            done = reduce(1, n, a, by_up)
            done = reduce(0, n, after(a, done), by_gate)
            if n:
                by_a = dot(after(by_gate, done), w_gate[n], ((1,), (1,))).astype(BF16).astype(F32)
                by_a = (by_a + dot(by_up, w_up[n], ((1,), (1,))).astype(BF16).astype(F32)).astype(BF16).astype(F32)
                wide, scale = h.astype(F32), scale_of(h)
                inner = jnp.sum(by_a * wide, -1, keepdims=True) / wide.shape[-1]
                by = by + (scale * by_a - wide * (scale**3 * inner)).astype(BF16)

        new = [None] * 3
        for which, layer, own, far in waiting:
            far = after(far, done)
            total = lax.optimization_barrier((own.astype(F32) + far.astype(F32)).astype(BF16))
            other = lax.ppermute(total, "dp", PARTNER)
            new[which] = adamw(mine, total, weights[which], m[which], v[which], layer, which < 2, new[which])
            new[which] = adamw(others, other, weights[which], m[which], v[which], layer, which < 2, new[which])
            done = new[which][0]
        return tuple(new[i][which] for which in range(3) for i in range(3))

    return jax.shard_map(
        step,
        mesh=mesh,
        in_specs=(P(("rep", "dp"), None, None),) * 2 + (P(None, None, None),) * 9,
        out_specs=(P("rep", None, None),) * 9,
        check_vma=False,
    )
```

time: 1890 us -> 1430 us (0.76)
  waiting for transfers between devices: 1080 us -> 494 us
  Pallas kernels: 0 us -> 273 us
  other arithmetic: 248 us -> 66.2 us
  matrix products: 519 us -> 542 us
    psum x1 -> x0, waiting for transfers between devices: 1080 us -> none  [step(): summed[number] = [lax.psum(by_w[name], 'dp') for name in NAMES]]
    ppermute x0 -> x18, waiting for transfers between devices: none -> 494 us  [the longest x6 463 us: reduce(): far = lax.ppermute(own, 'dp', ACROSS)]
    pallas_call x0 -> x12, Pallas kernels: none -> 273 us  [adamw(): pl.pallas_call(adamw_kernel, grid_spec=pltpu.PrefetchScalarGridSpec(num_s...]
    convert_element_type x2 -> x8, other arithmetic: 232 us -> 53.2 us  [the longest x6 43.9 us: step(): (own.astype(F32) + far.astype(F32)).astype(BF16)]
    dot_general x15 -> x21, matrix products: 519 us -> 542 us  [dot(): return lax.dot_general(a, b, (dims, ((), ())), preferred_element_type=F32)]
  transfers between devices with their start and end apart: 1 -> 18, of which waited for: 1 -> 11; matrix products, arithmetic and copies ran while one was open for 0% -> 3% of each run, Pallas kernels for 0% -> 18%
where the time goes in v1:
time: 1430 us; the launch traced here: 1420 us
  matrix products  542 us (38%)
  waiting for transfers between devices  494 us (35%)
  Pallas kernels  273 us (19%)
  other arithmetic  66.2 us (5%)
  local copies, waits for them, and re-layouts  30.1 us (2%)
    dot_general x21, matrix products, dot(): return lax.dot_general(a, b, (dims, ((), ())), preferred_element_type=F32)  542 us
    ppermute x6, waiting for transfers between devices, reduce(): far = lax.ppermute(own, 'dp', ACROSS)  463 us
    pallas_call x12, Pallas kernels, adamw(): pl.pallas_call(adamw_kernel, grid_spec=pltpu.PrefetchScalarGridSpec(num_s...  273 us
    convert_element_type x6, other arithmetic, step(): (own.astype(F32) + far.astype(F32)).astype(BF16)  43.9 us
    ppermute x6, waiting for transfers between devices, reduce(): got = lax.ppermute(first, 'dp', PARTNER)  31.1 us
  transfers between devices with their start and end apart: 18, of which 11 were waited for; matrix products, arithmetic and copies ran while one was open for 3% of the time, Pallas kernels for 18%

profile of v1, /device:TPU:0, one launch (start us, length us, event | category | flops | bytes accessed | tf_op | source)
XLA Modules:
  0.0 1419.8 jit_solution(14530328130888524662)
XLA Ops:
  0.7 8.6 copy.47
  9.3 4.1 fusion.8
  13.4 31.7 %fusion.29 = f32[2048,3584]{1,0:T(8,128)} fusion(bf16[2,1536,3584]{2,1,0:T(8,128)(2,1)} %w.23, bf16[1,2048,1536]{2,1,0:T(8,128)(2,1)} %param.11, f32[2048]{0:T(1024)S(1)} %add_rsqrt_fusion.1), kind=kOutput, calls=%fused_computation.48 | convolution fusion | flops 22558015488 | bytes 46669824 | tf_op jit(solution)/shard_map/dot_general | solution.py:15
  45.1 40.1 %multiply_convert_fusion.1 = (bf16[2048,3584]{1,0:T(8,128)(2,1)}, f32[2048,3584]{1,0:T(8,128)}) fusion(f32[2048,3584]{1,0:T(8,128)} %fusion.29, bf16[2,1536,3584]{2,1,0:T(8,128)(2,1)} %w.21, bf16[1,2048,1536]{2,1,0:T(8,128)(2,1)} %param.11, f32[2048]{0:T(1024)S(1)} %add_rsqrt_fusion.1), kind=kOutput, calls=%fused_computation.13 | convolution fusion | flops 22602055680 | bytes 90710016 | tf_op jit(solution)/shard_map/dot_general | solution.py:15
  85.3 32.2 %fusion.12 = (f32[2048]{0:T(1024)S(1)}, bf16[2048,1536]{0,1:T(8,128)(2,1)}) fusion(bf16[2048,3584]{1,0:T(8,128)(2,1)} %get-tuple-element.131, bf16[2,3584,1536]{2,1,0:T(8,128)(2,1)} %w.19, bf16[1,2048,1536]{1,2,0:T(8,128)(2,1)} %copy.47), kind=kOutput, calls=%fused_computation.29 | convolution fusion | flops 22564304896 | bytes 38281216 | tf_op jit(solution)/shard_map/dot_general | solution.py:15
  118.1 4.7 fusion.13
  122.8 2.7 copy-done
  125.4 30.2 %fusion.22 = f32[2048,3584]{1,0:T(8,128)} fusion(bf16[2048,1536]{0,1:T(8,128)(2,1)S(1)} %fusion.13, bf16[2,1536,3584]{2,1,0:T(8,128)(2,1)} %w.23), kind=kOutput, calls=%fused_computation.41 | convolution fusion | flops 22548578304 | bytes 46661632 | tf_op jit(solution)/shard_map/dot_general | solution.py:15
  155.6 39.8 %multiply_convert_fusion = (bf16[2048,3584]{1,0:T(8,128)(2,1)}, f32[2048,3584]{1,0:T(8,128)}) fusion(f32[2048,3584]{1,0:T(8,128)} %fusion.22, bf16[2048,1536]{0,1:T(8,128)(2,1)} %copy-done, bf16[2,1536,3584]{2,1,0:T(8,128)(2,1)} %w.21), kind=kOutput, calls=%fused_computation.10 | convolution fusion | flops 22592618496 | bytes 90701824 | tf_op jit(solution)/shard_map/dot_general | solution.py:15
  195.4 17.7 %convolution_convert_fusion.13 = bf16[3584,768]{1,0:T(8,128)(2,1)} fusion(bf16[2048,3584]{1,0:T(8,128)(2,1)} %get-tuple-element.135, bf16[1,2048,1536]{2,1,0:T(8,128)(2,1)} %param.12, s32[]{:T(128)S(6)} %select_n.13), kind=kOutput, calls=%fused_computation.85 | convolution fusion | flops 11277041664 | bytes 23330820 | tf_op jit(solution)/shard_map/dot_general | solution.py:15
  213.9 8.7 copy.48
  222.6 2.1 dynamic-slice_bitcast_fusion
  224.7 18.1 %add_convert_fusion.12 = bf16[3584,768]{1,0:T(8,128)(2,1)} fusion(bf16[3584,768]{1,0:T(8,128)(2,1)} %collective-permute-done, bf16[2048,3584]{1,0:T(8,128)(2,1)} %get-tuple-element.135, bf16[2048,768]{1,0:T(8,128)(2,1)S(1)} %dynamic-slice_bitcast_fusion), kind=kOutput, calls=%fused_computation.62 | convolution fusion | flops 11288051712 | bytes 28835840 | tf_op jit(solution)/shard_map/dot_general | solution.py:15
  242.8 48.1 %fusion.2 = (bf16[2048,3584]{1,0:T(8,128)(2,1)}, bf16[2048,3584]{1,0:T(8,128)(2,1)}) fusion(f32[2048,3584]{1,0:T(8,128)} %get-tuple-element.136, f32[2048,3584]{1,0:T(8,128)} %fusion.22, bf16[2048,1536]{0,1:T(8,128)(2,1)} %bitcast.98, bf16[2,3584,1536]{2,1,0:T(8,128)(2,1)} %w.19), kind=kOutput, calls=%fused_computation.6 | convolution fusion | flops 22658678784 | bytes 105381888 | tf_op jit(solution)/shard_map/dot_general | solution.py:15
  290.9 17.2 %convolution_convert_fusion.11 = bf16[768,3584]{1,0:T(8,128)(2,1)} fusion(bf16[2048,3584]{1,0:T(8,128)(2,1)} %get-tuple-element.72, bf16[2048,1536]{0,1:T(8,128)(2,1)} %copy-done, s32[]{:T(128)S(6)} %select_n.13), kind=kOutput, calls=%fused_computation.83 | convolution fusion | flops 11277041664 | bytes 23330820 | tf_op jit(solution)/shard_map/dot_general | solution.py:15
  308.1 2.3 constant_dynamic-slice_fusion.4
  310.4 7.0 collective-permute-done.1
  317.3 16.6 %add_convert_fusion.11 = bf16[768,3584]{1,0:T(8,128)(2,1)} fusion(bf16[768,3584]{1,0:T(8,128)(2,1)S(1)} %collective-permute-done.1, bf16[2048,768]{0,1:T(8,128)(2,1)S(1)} %constant_dynamic-slice_fusion.4, bf16[2048,3584]{1,0:T(8,128)(2,1)} %get-tuple-element.72), kind=kOutput, calls=%fused_computation.60 | convolution fusion | flops 11288051712 | bytes 28835840 | tf_op jit(solution)/shard_map/dot_general | solution.py:15
  333.9 16.4 %convolution_convert_fusion.9 = bf16[768,3584]{1,0:T(8,128)(2,1)} fusion(bf16[2048,3584]{1,0:T(8,128)(2,1)} %get-tuple-element.76, bf16[2048,1536]{0,1:T(8,128)(2,1)S(1)} %bitcast.100, s32[]{:T(128)S(6)} %select_n.13), kind=kOutput, calls=%fused_computation.81 | convolution fusion | flops 11277041664 | bytes 23330820 | tf_op jit(solution)/shard_map/dot_general | solution.py:15
  350.8 8.7 collective-permute-done.2
  359.5 16.7 %add_convert_fusion.10 = bf16[768,3584]{1,0:T(8,128)(2,1)} fusion(bf16[768,3584]{1,0:T(8,128)(2,1)S(1)} %collective-permute-done.2, bf16[2048,768]{0,1:T(8,128)(2,1)S(1)} %constant_dynamic-slice_fusion.3, bf16[2048,3584]{1,0:T(8,128)(2,1)} %get-tuple-element.76), kind=kOutput, calls=%fused_computation.59 | convolution fusion | flops 11288051712 | bytes 28835840 | tf_op jit(solution)/shard_map/dot_general | solution.py:15
  376.2 30.1 %fusion.43 = bf16[2048,1536]{0,1:T(8,128)(2,1)} fusion(bf16[2048,3584]{1,0:T(8,128)(2,1)} %get-tuple-element.76, bf16[2,1536,3584]{2,1,0:T(8,128)(2,1)} %w.23), kind=kOutput, calls=%fused_computation.72 | convolution fusion | flops 22551724032 | bytes 31981568 | tf_op jit(solution)/shard_map/dot_general | solution.py:15
  406.3 33.2 %fusion.14 = (f32[2048]{0:T(1024)S(1)}, bf16[2048,1536]{0,1:T(8,128)(2,1)}) fusion(bf16[2048,1536]{0,1:T(8,128)(2,1)} %get-tuple-element.134, bf16[2048,3584]{1,0:T(8,128)(2,1)} %get-tuple-element.72, bf16[2,1536,3584]{2,1,0:T(8,128)(2,1)} %w.21, bf16[2048,1536]{0,1:T(8,128)(2,1)} %fusion.43), kind=kOutput, calls=%fused_computation.31 | convolution fusion | flops 22576887808 | bytes 44572672 | tf_op jit(solution)/shard_map/dot_general | solution.py:15
  439.6 8.8 fusion.50
  448.4 19.2 %convolution_convert_fusion.7 = bf16[3584,768]{1,0:T(8,128)(2,1)} fusion(bf16[2048,3584]{1,0:T(8,128)(2,1)} %get-tuple-element.131, bf16[2048,1536]{0,1:T(8,128)(2,1)S(1)} %fusion.50, s32[]{:T(128)S(6)} %select_n.13), kind=kOutput, calls=%fused_computation.79 | convolution fusion | flops 11277041664 | bytes 23330820 | tf_op jit(solution)/shard_map/dot_general | solution.py:15
  467.8 4.6 fusion.9
  472.8 4.2 collective-permute-done.3
  477.0 17.6 %add_convert_fusion.9 = bf16[3584,768]{1,0:T(8,128)(2,1)} fusion(bf16[3584,768]{1,0:T(8,128)(2,1)} %collective-permute-done.3, bf16[2048,3584]{1,0:T(8,128)(2,1)} %get-tuple-element.131, bf16[2048,768]{0,1:T(8,128)(2,1)S(1)} %constant_dynamic-slice_fusion.2), kind=kOutput, calls=%fused_computation.58 | convolution fusion | flops 11288051712 | bytes 28835840 | tf_op jit(solution)/shard_map/dot_general | solution.py:15
  494.7 48.2 %fusion.5 = (bf16[2048,3584]{1,0:T(8,128)(2,1)}, bf16[2048,3584]{1,0:T(8,128)(2,1)}) fusion(f32[2048,3584]{1,0:T(8,128)} %get-tuple-element.132, f32[2048,3584]{1,0:T(8,128)} %fusion.29, bf16[2048,1536]{0,1:T(8,128)(2,1)} %copy-done.1, bf16[2,3584,1536]{2,1,0:T(8,128)(2,1)} %w.19), kind=kOutput, calls=%fused_computation.9 | convolution fusion | flops 22658678784 | bytes 105381888 | tf_op jit(solution)/shard_map/dot_general | solution.py:15
  542.8 17.2 %convolution_convert_fusion.5 = bf16[768,3584]{1,0:T(8,128)(2,1)} fusion(bf16[2048,3584]{1,0:T(8,128)(2,1)} %get-tuple-element.80, bf16[2048,1536]{0,1:T(8,128)(2,1)} %fusion.9, s32[]{:T(128)S(6)} %select_n.13), kind=kOutput, calls=%fused_computation.77 | convolution fusion | flops 11277041664 | bytes 23330820 | tf_op jit(solution)/shard_map/dot_general | solution.py:15
  560.2 2.4 constant_dynamic-slice_fusion.1
  562.7 6.7 collective-permute-done.4
  569.4 17.6 %add_convert_fusion.8 = bf16[768,3584]{1,0:T(8,128)(2,1)} fusion(bf16[768,3584]{1,0:T(8,128)(2,1)} %collective-permute-done.4, bf16[2048,768]{0,1:T(8,128)(2,1)S(1)} %constant_dynamic-slice_fusion.1, bf16[2048,3584]{1,0:T(8,128)(2,1)} %get-tuple-element.80), kind=kOutput, calls=%fused_computation.57 | convolution fusion | flops 11288051712 | bytes 28835840 | tf_op jit(solution)/shard_map/dot_general | solution.py:15
  587.0 16.4 %convolution_convert_fusion.3 = bf16[768,3584]{1,0:T(8,128)(2,1)} fusion(bf16[2048,3584]{1,0:T(8,128)(2,1)} %get-tuple-element.83, bf16[2048,1536]{0,1:T(8,128)(2,1)S(1)} %bitcast.102, s32[]{:T(128)S(6)} %select_n.13), kind=kOutput, calls=%fused_computation.75 | convolution fusion | flops 11277041664 | bytes 23330820 | tf_op jit(solution)/shard_map/dot_general | solution.py:15
  603.5 2.8 collective-permute-start.11
  606.4 1.9 constant_dynamic-slice_fusion
  608.3 4.5 collective-permute-done.5
  612.7 18.2 %add_convert_fusion.7 = bf16[768,3584]{1,0:T(8,128)(2,1)} fusion(bf16[768,3584]{1,0:T(8,128)(2,1)} %collective-permute-done.5, bf16[2048,768]{0,1:T(8,128)(2,1)} %constant_dynamic-slice_fusion, bf16[2048,3584]{1,0:T(8,128)(2,1)} %get-tuple-element.83), kind=kOutput, calls=%fused_computation.56 | convolution fusion | flops 11288051712 | bytes 28835840 | tf_op jit(solution)/shard_map/dot_general | solution.py:15
  631.0 94.4 %collective-permute-done.11 = bf16[3584,768]{1,0:T(8,128)(2,1)S(1)} collective-permute-done((bf16[3584,768]{1,0:T(8,128)(2,1)S(1)}, bf16[3584,768]{1,0:T(8,128)(2,1)S(1)}, u32[]{:S(2)}, u32[]{:S(2)}) %collective-permute-start.11) | collective-permute-done | bytes 5505056 | tf_op jit(solution)/shard_map/ppermute | solution.py:97
  725.3 3.8 add_convert_fusion.6.g
  730.9 24.8 %adamw.12 = (bf16[2,3584,1536]{2,1,0:T(8,128)(2,1)}, f32[2,3584,1536]{2,1,0:T(8,128)}, f32[2,3584,1536]{2,1,0:T(8,128)}) custom-call(s32[1]{0:T(128)} %bitcast.12.side, bf16[3584,768]{1,0:T(8,128)(2,1)} %add_convert_fusion.6.g, bf16[2,3584,1536]{2,1,0:T(8,128)(2,1)} %w.19, f32[2,3584,1536]{2,1,0:T(8,128)} %m.19, f32[2,3584,1536]{2,1,0:T(8,128)} %v.19), custom_call_target="tpu_custom_call" | custom-call | flops 11010048000 | bytes 60555264 | tf_op jit(solution)/shard_map/adamw/pallas_call | solution.py:48
  755.7 24.8 %adamw.13 = (bf16[2,3584,1536]{2,1,0:T(8,128)(2,1)}, f32[2,3584,1536]{2,1,0:T(8,128)}, f32[2,3584,1536]{2,1,0:T(8,128)}) custom-call(s32[1]{0:T(128)} %bitcast.side, bf16[3584,768]{1,0:T(8,128)(2,1)} %collective-permute-done.12.g, bf16[2,3584,1536]{2,1,0:T(8,128)(2,1)} %w.19, ...), custom_call_target="tpu_custom_call", output_to_operand_aliasing={{0}: (5, {}), {1}: (6, {}), {2}: (7, {})} | custom-call | flops 11010048000 | bytes 60555264 | tf_op jit(solution)/shard_map/adamw/pallas_call | solution.py:48
  780.5 70.0 %collective-permute-done.10 = bf16[768,3584]{1,0:T(8,128)(2,1)} collective-permute-done((bf16[768,3584]{1,0:T(8,128)(2,1)}, bf16[768,3584]{1,0:T(8,128)(2,1)}, u32[]{:S(2)}, u32[]{:S(2)}) %collective-permute-start.10) | collective-permute-done | bytes 5505056 | tf_op jit(solution)/shard_map/ppermute | solution.py:97
  850.6 8.1 add_convert_fusion.5.g
  860.4 21.6 %adamw.14 = (bf16[2,1536,3584]{2,1,0:T(8,128)(2,1)}, f32[2,1536,3584]{2,1,0:T(8,128)}, f32[2,1536,3584]{2,1,0:T(8,128)}) custom-call(s32[1]{0:T(128)} %bitcast.12.side, bf16[768,3584]{1,0:T(8,128)(2,1)} %add_convert_fusion.5.g, bf16[2,1536,3584]{2,1,0:T(8,128)(2,1)} %w.21, f32[2,1536,3584]{2,1,0:T(8,128)} %m.21, f32[2,1536,3584]{2,1,0:T(8,128)} %v.21), custom_call_target="tpu_custom_call" | custom-call | flops 11010048000 | bytes 60555264 | tf_op jit(solution)/shard_map/adamw/pallas_call | solution.py:48
  882.0 21.9 %adamw.15 = (bf16[2,1536,3584]{2,1,0:T(8,128)(2,1)}, f32[2,1536,3584]{2,1,0:T(8,128)}, f32[2,1536,3584]{2,1,0:T(8,128)}) custom-call(s32[1]{0:T(128)} %bitcast.side, bf16[768,3584]{1,0:T(8,128)(2,1)} %collective-permute-done.13.g, bf16[2,1536,3584]{2,1,0:T(8,128)(2,1)} %w.21, ...), custom_call_target="tpu_custom_call", output_to_operand_aliasing={{0}: (5, {}), {1}: (6, {}), {2}: (7, {})} | custom-call | flops 11010048000 | bytes 60555264 | tf_op jit(solution)/shard_map/adamw/pallas_call | solution.py:48
  903.9 76.1 %collective-permute-done.9 = bf16[768,3584]{1,0:T(8,128)(2,1)} collective-permute-done((bf16[768,3584]{1,0:T(8,128)(2,1)}, bf16[768,3584]{1,0:T(8,128)(2,1)}, u32[]{:S(2)}, u32[]{:S(2)}) %collective-permute-start.9) | collective-permute-done | bytes 5505056 | tf_op jit(solution)/shard_map/ppermute | solution.py:97
  980.0 8.0 add_convert_fusion.4.g
  988.1 1.7 collective-permute-start.8
  989.8 21.6 %adamw.16 = (bf16[2,1536,3584]{2,1,0:T(8,128)(2,1)}, f32[2,1536,3584]{2,1,0:T(8,128)}, f32[2,1536,3584]{2,1,0:T(8,128)}) custom-call(s32[1]{0:T(128)} %bitcast.12.side, bf16[768,3584]{1,0:T(8,128)(2,1)} %add_convert_fusion.4.g, bf16[2,1536,3584]{2,1,0:T(8,128)(2,1)} %w.23, f32[2,1536,3584]{2,1,0:T(8,128)} %m.23, f32[2,1536,3584]{2,1,0:T(8,128)} %v.23), custom_call_target="tpu_custom_call" | custom-call | flops 11010048000 | bytes 60555264 | tf_op jit(solution)/shard_map/adamw/pallas_call | solution.py:48
  1011.4 21.7 %adamw.17 = (bf16[2,1536,3584]{2,1,0:T(8,128)(2,1)}, f32[2,1536,3584]{2,1,0:T(8,128)}, f32[2,1536,3584]{2,1,0:T(8,128)}) custom-call(s32[1]{0:T(128)} %bitcast.side, bf16[768,3584]{1,0:T(8,128)(2,1)} %collective-permute-done.14.g, bf16[2,1536,3584]{2,1,0:T(8,128)(2,1)} %w.23, ...), custom_call_target="tpu_custom_call", output_to_operand_aliasing={{0}: (5, {}), {1}: (6, {}), {2}: (7, {})} | custom-call | flops 11010048000 | bytes 60555264 | tf_op jit(solution)/shard_map/adamw/pallas_call | solution.py:48
  1033.1 76.3 %collective-permute-done.8 = bf16[3584,768]{1,0:T(8,128)(2,1)} collective-permute-done((bf16[3584,768]{1,0:T(8,128)(2,1)}, bf16[3584,768]{1,0:T(8,128)(2,1)}, u32[]{:S(2)}, u32[]{:S(2)}) %collective-permute-start.8) | collective-permute-done | bytes 5505056 | tf_op jit(solution)/shard_map/ppermute | solution.py:97
  1109.4 8.0 add_convert_fusion.3.g
  1117.4 1.7 collective-permute-start.7
  1119.1 24.9 %adamw.18 = (bf16[2,3584,1536]{2,1,0:T(8,128)(2,1)}, f32[2,3584,1536]{2,1,0:T(8,128)}, f32[2,3584,1536]{2,1,0:T(8,128)}) custom-call(s32[1]{0:T(128)} %bitcast.12.side, bf16[3584,768]{1,0:T(8,128)(2,1)} %add_convert_fusion.3.g, bf16[2,3584,1536]{2,1,0:T(8,128)(2,1)} %w.19, ...), custom_call_target="tpu_custom_call", output_to_operand_aliasing={{0}: (5, {}), {1}: (6, {}), {2}: (7, {})} | custom-call | flops 11010048000 | bytes 60555264 | tf_op jit(solution)/shard_map/adamw/pallas_call | solution.py:48
  1144.0 24.9 %adamw.19 = (bf16[2,3584,1536]{2,1,0:T(8,128)(2,1)}, f32[2,3584,1536]{2,1,0:T(8,128)}, f32[2,3584,1536]{2,1,0:T(8,128)}) custom-call(s32[1]{0:T(128)} %bitcast.side, bf16[3584,768]{1,0:T(8,128)(2,1)} %collective-permute-done.15.g, bf16[2,3584,1536]{2,1,0:T(8,128)(2,1)} %w.19, ...), custom_call_target="tpu_custom_call", output_to_operand_aliasing={{0}: (5, {}), {1}: (6, {}), {2}: (7, {})} | custom-call | flops 11010048000 | bytes 60555264 | tf_op jit(solution)/shard_map/adamw/pallas_call | solution.py:48
  1169.0 69.8 %collective-permute-done.7 = bf16[768,3584]{1,0:T(8,128)(2,1)} collective-permute-done((bf16[768,3584]{1,0:T(8,128)(2,1)}, bf16[768,3584]{1,0:T(8,128)(2,1)}, u32[]{:S(2)}, u32[]{:S(2)}) %collective-permute-start.7) | collective-permute-done | bytes 5505056 | tf_op jit(solution)/shard_map/ppermute | solution.py:97
  1238.8 8.1 add_convert_fusion.2.g
  1248.6 21.6 %adamw.20 = (bf16[2,1536,3584]{2,1,0:T(8,128)(2,1)}, f32[2,1536,3584]{2,1,0:T(8,128)}, f32[2,1536,3584]{2,1,0:T(8,128)}) custom-call(s32[1]{0:T(128)} %bitcast.12.side, bf16[768,3584]{1,0:T(8,128)(2,1)} %add_convert_fusion.2.g, bf16[2,1536,3584]{2,1,0:T(8,128)(2,1)} %w.21, ...), custom_call_target="tpu_custom_call", output_to_operand_aliasing={{0}: (5, {}), {1}: (6, {}), {2}: (7, {})} | custom-call | flops 11010048000 | bytes 60555264 | tf_op jit(solution)/shard_map/adamw/pallas_call | solution.py:48
  1270.2 21.7 %adamw.21 = (bf16[2,1536,3584]{2,1,0:T(8,128)(2,1)}, f32[2,1536,3584]{2,1,0:T(8,128)}, f32[2,1536,3584]{2,1,0:T(8,128)}) custom-call(s32[1]{0:T(128)} %bitcast.side, bf16[768,3584]{1,0:T(8,128)(2,1)} %collective-permute-done.16.g, bf16[2,1536,3584]{2,1,0:T(8,128)(2,1)} %w.21, ...), custom_call_target="tpu_custom_call", output_to_operand_aliasing={{0}: (5, {}), {1}: (6, {}), {2}: (7, {})} | custom-call | flops 11010048000 | bytes 60555264 | tf_op jit(solution)/shard_map/adamw/pallas_call | solution.py:48
  1291.9 76.3 %collective-permute-done.6 = bf16[768,3584]{1,0:T(8,128)(2,1)} collective-permute-done((bf16[768,3584]{1,0:T(8,128)(2,1)}, bf16[768,3584]{1,0:T(8,128)(2,1)}, u32[]{:S(2)}, u32[]{:S(2)}) %collective-permute-start.6) | collective-permute-done | bytes 5505056 | tf_op jit(solution)/shard_map/ppermute | solution.py:97
  1368.2 8.0 add_convert_fusion.1.g
  1376.3 21.7 %adamw.22 = (bf16[2,1536,3584]{2,1,0:T(8,128)(2,1)}, f32[2,1536,3584]{2,1,0:T(8,128)}, f32[2,1536,3584]{2,1,0:T(8,128)}) custom-call(s32[1]{0:T(128)} %bitcast.12.side, bf16[768,3584]{1,0:T(8,128)(2,1)} %add_convert_fusion.1.g, bf16[2,1536,3584]{2,1,0:T(8,128)(2,1)} %w.23, ...), custom_call_target="tpu_custom_call", output_to_operand_aliasing={{0}: (5, {}), {1}: (6, {}), {2}: (7, {})} | custom-call | flops 11010048000 | bytes 60555264 | tf_op jit(solution)/shard_map/adamw/pallas_call | solution.py:48
  1397.9 21.7 %adamw.23 = (bf16[2,1536,3584]{2,1,0:T(8,128)(2,1)}, f32[2,1536,3584]{2,1,0:T(8,128)}, f32[2,1536,3584]{2,1,0:T(8,128)}) custom-call(s32[1]{0:T(128)} %bitcast.side, bf16[768,3584]{1,0:T(8,128)(2,1)} %collective-permute-done.17.g, bf16[2,1536,3584]{2,1,0:T(8,128)(2,1)} %w.23, ...), custom_call_target="tpu_custom_call", output_to_operand_aliasing={{0}: (5, {}), {1}: (6, {}), {2}: (7, {})} | custom-call | flops 11010048000 | bytes 60555264 | tf_op jit(solution)/shard_map/adamw/pallas_call | solution.py:48
  (62 shorter events, 8.2 us)
Async XLA Ops:
  13.4 31.8 %copy-start.6 = (f32[2048]{0:T(1024)}, f32[2048]{0:T(1024)S(1)}, u32[]{:S(2)}) copy-start(f32[2048]{0:T(1024)S(1)} %add_rsqrt_fusion.1) | copy-start | bytes 24580
  117.5 38.2 %copy-start.4 = (f32[2048]{0:T(1024)}, f32[2048]{0:T(1024)S(1)}, u32[]{:S(2)}) copy-start(f32[2048]{0:T(1024)S(1)} %get-tuple-element.133) | copy-start | bytes 24580
  117.5 0.6 copy-start.2
  122.8 2.7 copy-start
  213.1 11.6 collective-permute-start
  308.1 9.2 collective-permute-start.1
  308.1 25.8 %slice-start.2 = ((s8[6291456]{0:T(1024)(128)(4,1)}), s8[4194304]{0:T(1024)(128)(4,1)S(1)}, s32[]{:S(2)}) async-start(s8[6291456]{0:T(1024)(128)(4,1)} %bitcast.99), calls=%async_computation.2 | async-start | bytes 8388608
  310.4 23.6 %slice-start.3 = ((s8[6291456]{0:T(1024)(128)(4,1)}), s8[2097152]{0:T(1024)(128)(4,1)S(1)}, s32[]{:S(2)}) async-start(s8[6291456]{0:T(1024)(128)(4,1)} %bitcast.99), calls=%async_computation.3 | async-start | bytes 4194304
  350.3 9.2 collective-permute-start.2
  406.3 33.2 %copy-start.5 = (f32[2048]{0:T(1024)S(1)}, f32[2048]{0:T(1024)}, u32[]{:S(2)}) copy-start(f32[2048]{0:T(1024)} %copy-done.4) | copy-start | bytes 24580
  406.3 33.2 %copy-start.3 = (f32[2048]{0:T(1024)S(1)}, f32[2048]{0:T(1024)}, u32[]{:S(2)}) copy-start(f32[2048]{0:T(1024)} %copy-done.2) | copy-start | bytes 24580
  439.5 28.3 %slice-start = ((s8[6291456]{0:T(1024)(128)(4,1)}), s8[4194304]{0:T(1024)(128)(4,1)S(1)}, s32[]{:S(2)}) async-start(s8[6291456]{0:T(1024)(128)(4,1)} %bitcast.96), calls=%async_computation | async-start | bytes 8388608
  448.4 24.0 %copy-start.1 = (bf16[2048,1536]{0,1:T(8,128)(2,1)}, bf16[2048,1536]{0,1:T(8,128)(2,1)S(1)}, u32[]{:S(2)}) copy-start(bf16[2048,1536]{0,1:T(8,128)(2,1)S(1)} %fusion.50) | copy-start | bytes 18874372
  448.4 19.4 %slice-start.1 = ((s8[6291456]{0:T(1024)(128)(4,1)}), s8[2097152]{0:T(1024)(128)(4,1)S(1)}, s32[]{:S(2)}) async-start(s8[6291456]{0:T(1024)(128)(4,1)} %bitcast.96), calls=%async_computation.1 | async-start | bytes 4194304
  448.4 19.4 %copy-start.7 = (f32[2048]{0:T(1024)S(1)}, f32[2048]{0:T(1024)}, u32[]{:S(2)}) copy-start(f32[2048]{0:T(1024)} %copy-done.6) | copy-start | bytes 24580
  467.7 9.4 collective-permute-start.3
  560.0 9.4 collective-permute-start.4
  560.2 26.8 %slice-start.4 = ((s8[6291456]{0:T(1024)(128)(4,1)}), s8[4194304]{0:T(1024)(128)(4,1)S(1)}, s32[]{:S(2)}) async-start(s8[6291456]{0:T(1024)(128)(4,1)} %bitcast.101), calls=%async_computation.4 | async-start | bytes 8388608
  560.2 43.3 %slice-start.6 = ((s8[5505024]{0:T(1024)(128)(4,1)}), s8[4194304]{0:T(1024)(128)(4,1)S(1)}, s32[]{:S(2)}) async-start(s8[5505024]{0:T(1024)(128)(4,1)} %bitcast.103), calls=%async_computation.6 | async-start | bytes 8388608
  562.7 24.3 %slice-start.5 = ((s8[6291456]{0:T(1024)(128)(4,1)}), s8[2097152]{0:T(1024)(128)(4,1)S(1)}, s32[]{:S(2)}) async-start(s8[6291456]{0:T(1024)(128)(4,1)} %bitcast.101), calls=%async_computation.5 | async-start | bytes 4194304
  562.7 40.9 %slice-start.7 = ((s8[5505024]{0:T(1024)(128)(4,1)}), s8[1310720]{0:T(1024)(128)(4,1)S(1)}, s32[]{:S(2)}) async-start(s8[5505024]{0:T(1024)(128)(4,1)} %bitcast.103), calls=%async_computation.7 | async-start | bytes 2621440
  603.4 9.4 collective-permute-start.5
  603.5 121.8 %collective-permute-start.11 = (bf16[3584,768]{1,0:T(8,128)(2,1)S(1)}, bf16[3584,768]{1,0:T(8,128)(2,1)S(1)}, u32[]{:S(2)}, u32[]{:S(2)}) collective-permute-start(bf16[3584,768]{1,0:T(8,128)(2,1)S(1)} %bitcast.104), channel_id=1, source_target_pairs={{0,2},{2,0},{1,3},{3,1},{4,6},{6,4},{5,7},{7,5}} | collective-permute-start | bytes 16515080 | tf_op jit(solution)/shard_map/ppermute | solution.py:97
  729.2 26.5 %collective-permute-start.12 = (bf16[3584,768]{1,0:T(8,128)(2,1)}, bf16[3584,768]{1,0:T(8,128)(2,1)}, u32[]{:S(2)}, u32[]{:S(2)}) collective-permute-start(bf16[3584,768]{1,0:T(8,128)(2,1)} %add_convert_fusion.6.g), channel_id=1, source_target_pairs={{0,1},{1,0},{2,3},{3,2},{4,5},{5,4},{6,7},{7,6}} | collective-permute-start | bytes 16515080 | tf_op jit(solution)/shard_map/ppermute | solution.py:123
  729.2 121.4 %collective-permute-start.10 = (bf16[768,3584]{1,0:T(8,128)(2,1)}, bf16[768,3584]{1,0:T(8,128)(2,1)}, u32[]{:S(2)}, u32[]{:S(2)}) collective-permute-start(bf16[768,3584]{1,0:T(8,128)(2,1)} %add_convert_fusion.11), channel_id=1, source_target_pairs={{0,2},{2,0},{1,3},{3,1},{4,6},{6,4},{5,7},{7,5}} | collective-permute-start | bytes 16515080 | tf_op jit(solution)/shard_map/ppermute | solution.py:97
  858.6 23.4 %collective-permute-start.13 = (bf16[768,3584]{1,0:T(8,128)(2,1)}, bf16[768,3584]{1,0:T(8,128)(2,1)}, u32[]{:S(2)}, u32[]{:S(2)}) collective-permute-start(bf16[768,3584]{1,0:T(8,128)(2,1)} %add_convert_fusion.5.g), channel_id=1, source_target_pairs={{0,1},{1,0},{2,3},{3,2},{4,5},{5,4},{6,7},{7,6}} | collective-permute-start | bytes 16515080 | tf_op jit(solution)/shard_map/ppermute | solution.py:123
  858.6 121.4 %collective-permute-start.9 = (bf16[768,3584]{1,0:T(8,128)(2,1)}, bf16[768,3584]{1,0:T(8,128)(2,1)}, u32[]{:S(2)}, u32[]{:S(2)}) collective-permute-start(bf16[768,3584]{1,0:T(8,128)(2,1)} %add_convert_fusion.10), channel_id=1, source_target_pairs={{0,2},{2,0},{1,3},{3,1},{4,6},{6,4},{5,7},{7,5}} | collective-permute-start | bytes 16515080 | tf_op jit(solution)/shard_map/ppermute | solution.py:97
  988.1 23.4 %collective-permute-start.14 = (bf16[768,3584]{1,0:T(8,128)(2,1)}, bf16[768,3584]{1,0:T(8,128)(2,1)}, u32[]{:S(2)}, u32[]{:S(2)}) collective-permute-start(bf16[768,3584]{1,0:T(8,128)(2,1)} %add_convert_fusion.4.g), channel_id=1, source_target_pairs={{0,1},{1,0},{2,3},{3,2},{4,5},{5,4},{6,7},{7,6}} | collective-permute-start | bytes 16515080 | tf_op jit(solution)/shard_map/ppermute | solution.py:123
  988.1 121.4 %collective-permute-start.8 = (bf16[3584,768]{1,0:T(8,128)(2,1)}, bf16[3584,768]{1,0:T(8,128)(2,1)}, u32[]{:S(2)}, u32[]{:S(2)}) collective-permute-start(bf16[3584,768]{1,0:T(8,128)(2,1)} %add_convert_fusion.9), channel_id=1, source_target_pairs={{0,2},{2,0},{1,3},{3,1},{4,6},{6,4},{5,7},{7,5}} | collective-permute-start | bytes 16515080 | tf_op jit(solution)/shard_map/ppermute | solution.py:97
  1117.4 26.6 %collective-permute-start.15 = (bf16[3584,768]{1,0:T(8,128)(2,1)}, bf16[3584,768]{1,0:T(8,128)(2,1)}, u32[]{:S(2)}, u32[]{:S(2)}) collective-permute-start(bf16[3584,768]{1,0:T(8,128)(2,1)} %add_convert_fusion.3.g), channel_id=1, source_target_pairs={{0,1},{1,0},{2,3},{3,2},{4,5},{5,4},{6,7},{7,6}} | collective-permute-start | bytes 16515080 | tf_op jit(solution)/shard_map/ppermute | solution.py:123
  1117.4 121.4 %collective-permute-start.7 = (bf16[768,3584]{1,0:T(8,128)(2,1)}, bf16[768,3584]{1,0:T(8,128)(2,1)}, u32[]{:S(2)}, u32[]{:S(2)}) collective-permute-start(bf16[768,3584]{1,0:T(8,128)(2,1)} %add_convert_fusion.8), channel_id=1, source_target_pairs={{0,2},{2,0},{1,3},{3,1},{4,6},{6,4},{5,7},{7,5}} | collective-permute-start | bytes 16515080 | tf_op jit(solution)/shard_map/ppermute | solution.py:97
  1246.9 23.4 %collective-permute-start.16 = (bf16[768,3584]{1,0:T(8,128)(2,1)}, bf16[768,3584]{1,0:T(8,128)(2,1)}, u32[]{:S(2)}, u32[]{:S(2)}) collective-permute-start(bf16[768,3584]{1,0:T(8,128)(2,1)} %add_convert_fusion.2.g), channel_id=1, source_target_pairs={{0,1},{1,0},{2,3},{3,2},{4,5},{5,4},{6,7},{7,6}} | collective-permute-start | bytes 16515080 | tf_op jit(solution)/shard_map/ppermute | solution.py:123
  1246.9 121.4 %collective-permute-start.6 = (bf16[768,3584]{1,0:T(8,128)(2,1)}, bf16[768,3584]{1,0:T(8,128)(2,1)}, u32[]{:S(2)}, u32[]{:S(2)}) collective-permute-start(bf16[768,3584]{1,0:T(8,128)(2,1)} %add_convert_fusion.7), channel_id=1, source_target_pairs={{0,2},{2,0},{1,3},{3,1},{4,6},{6,4},{5,7},{7,5}} | collective-permute-start | bytes 16515080 | tf_op jit(solution)/shard_map/ppermute | solution.py:97
  1376.3 21.7 %collective-permute-start.17 = (bf16[768,3584]{1,0:T(8,128)(2,1)}, bf16[768,3584]{1,0:T(8,128)(2,1)}, u32[]{:S(2)}, u32[]{:S(2)}) collective-permute-start(bf16[768,3584]{1,0:T(8,128)(2,1)} %add_convert_fusion.1.g), channel_id=1, source_target_pairs={{0,1},{1,0},{2,3},{3,2},{4,5},{5,4},{6,7},{7,6}} | collective-permute-start | bytes 16515080 | tf_op jit(solution)/shard_map/ppermute | solution.py:123

commit v2 on v0

v2 whole, which is shorter than its diff:
```python
import functools

import jax
import jax.numpy as jnp
from jax import lax
from jax.experimental import pallas as pl
from jax.experimental.pallas import tpu as pltpu
from jax.sharding import PartitionSpec as P


F32, BF16 = jnp.float32, jnp.bfloat16
PARTNER = [(0, 1), (1, 0), (2, 3), (3, 2)]
ACROSS = [(0, 2), (2, 0), (1, 3), (3, 1)]
GATE, UP, DOWN = range(3)
TILE = 256
ROWS = {"forward": 1024, "turn": 1024, "back": 2048}
MIB = {"forward": 62, "turn": 62, "back": 62, "term": 62, "adamw": 62}
ANY = pl.BlockSpec(memory_space=pl.ANY)


def dot(a, b, dims):
    return lax.dot_general(a, b, (dims, ((), ())), preferred_element_type=F32)


def fixed(shape, where=None):
    return pl.BlockSpec(shape, where or (lambda j, s: (0,) * len(shape)), pipeline_mode=pl.Buffered(1))


def cost(flops, moved):
    return pl.CostEstimate(flops=int(flops), bytes_accessed=int(moved), transcendentals=0)


def norm_into(h_ref, a_ref):
    @pl.when(pl.program_id(0) == 0)
    def _():
        @pl.loop(0, h_ref.shape[0], step=TILE)
        def _(r):
            wide = h_ref[pl.ds(r, TILE), :].astype(F32)
            scale = lax.rsqrt(jnp.mean(wide * wide, -1, keepdims=True) + 1e-6)
            a_ref[pl.ds(r, TILE), :] = (wide * scale).astype(BF16)


def forward_kernel(_, h, w_gate, w_up, a, hidden, gate, up):
    norm_into(h, a)
    for r in range(0, h.shape[0], ROWS["forward"]):
        rows = slice(r, r + ROWS["forward"])
        g, u = dot(a[rows], w_gate[0], ((1,), (0,))), dot(a[rows], w_up[0], ((1,), (0,)))
        gate[rows], up[rows] = g, u
        hidden[rows] = (g * jax.nn.sigmoid(g) * u).astype(BF16)


def backward(by_hidden, g, u):
    by_hidden = by_hidden.astype(BF16).astype(F32)
    sig = jax.nn.sigmoid(g)
    silu = g * sig
    return (by_hidden * u * (sig + silu * (1 - sig))).astype(BF16), (by_hidden * silu).astype(BF16), (silu * u).astype(BF16)


def turn_kernel(_, h, by, w_gate, w_up, w_down, a, hidden, by_gate, by_up):
    norm_into(h, a)
    for r in range(0, h.shape[0], ROWS["turn"]):
        rows = slice(r, r + ROWS["turn"])
        g, u = dot(a[rows], w_gate[0], ((1,), (0,))), dot(a[rows], w_up[0], ((1,), (0,)))
        by_gate[rows], by_up[rows], hidden[rows] = backward(dot(by[rows], w_down[0], ((1,), (1,))), g, u)


def back_kernel(_, by, w_down, gate, up, by_gate, by_up):
    for r in range(0, by.shape[0], ROWS["back"]):
        rows = slice(r, r + ROWS["back"])
        by_gate[rows], by_up[rows], _ = backward(dot(by[rows], w_down[0], ((1,), (1,))), gate[rows], up[rows])


def call(kernel, name, scalars, tiles, ins, args, outs, shapes, flops, aliases={}):
    moved = sum(x.size * x.dtype.itemsize for x in shapes)
    return pl.pallas_call(
        kernel,
        grid_spec=pltpu.PrefetchScalarGridSpec(num_scalar_prefetch=1, grid=(tiles,), in_specs=ins, out_specs=outs),
        out_shape=shapes,
        input_output_aliases=aliases,
        cost_estimate=cost(flops, moved),
        compiler_params=pltpu.CompilerParams(vmem_limit_bytes=MIB[name] << 20),
    )(scalars, *args)


def weight_in(layer, d):
    return pl.BlockSpec((1, d, TILE), lambda j, s: (layer, 0, s[0] + j))


def weight_out(layer, d):
    return pl.BlockSpec((1, TILE, d), lambda j, s: (layer, s[0] + j, 0))


def shaped(*shape, dtype=BF16):
    return jax.ShapeDtypeStruct(shape, dtype)


def forward(h, w, layer, start):
    t, d = h.shape
    f = w[GATE].shape[-1]
    column = pl.BlockSpec((t, TILE), lambda j, s: (0, j))
    return call(
        forward_kernel, "forward", start, f // TILE,
        [fixed((t, d)), weight_in(layer, d), weight_in(layer, d)], (h, w[GATE], w[UP]),
        [fixed((t, d)), column, column, column],
        [shaped(t, d), shaped(t, f), shaped(t, f, dtype=F32), shaped(t, f, dtype=F32)], 4 * t * d * f,
    )


def turn(h, by, w, layer, start, f):
    t, d = h.shape
    column = pl.BlockSpec((t, TILE), lambda j, s: (0, j))
    return call(
        turn_kernel, "turn", start, f // TILE,
        [fixed((t, d)), fixed((t, d)), weight_in(layer, d), weight_in(layer, d), weight_out(layer, d)], (h, by, *w),
        [fixed((t, d)), column, column, column], [shaped(t, d)] + [shaped(t, f)] * 3, 6 * t * d * f,
    )


def back(by, w, gate, up, layer, start):
    t, d = by.shape
    f = gate.shape[-1]
    column = pl.BlockSpec((t, TILE), lambda j, s: (0, j))
    return call(
        back_kernel, "back", start, f // TILE, [fixed((t, d)), weight_out(layer, d), column, column], (by, w[DOWN], gate, up),
        [column, column], [shaped(t, f)] * 2, 2 * t * d * f,
    )


def term_kernel(pairs, added, _, *refs):
    ins, out = refs[:-1], refs[-1]
    total = None
    for n in range(pairs):
        part = dot(ins[2 * n][...], ins[2 * n + 1][...], ((0,), (0,)))
        total = part if total is None else total + part
    if added:
        total = total + ins[-1][...].astype(F32)
    out[...] = total.astype(BF16)


def term(where, pairs, m, n, tile, got=None, old=None, layer=None):
    t = pairs[0][0].shape[0]
    ins, args = [], []
    for i, (left, right) in enumerate(pairs):
        ins.append(fixed((t, m), functools.partial(lambda i, j, s: (0, s[i]), i)))
        ins.append(pl.BlockSpec((t, tile), functools.partial(lambda i, j, s: (0, s[i] + j), len(pairs) + i)))
        args += [left, right]
    out = pl.BlockSpec((m, tile), lambda j, s: (0, j))
    if got is not None:
        ins.append(out)
        args.append(got)
    scalars = jnp.stack([jnp.asarray(x, jnp.int32) for x in where])
    if old is not None:
        block = pl.BlockSpec((1, m, tile), lambda j, s: (layer, s[2 * len(pairs)], s[2 * len(pairs) + 1] + j))
        return call(
            functools.partial(last_term_kernel, len(pairs)), "term", scalars, n // tile, ins + [block] * 3, args + list(old), [out] + [block] * 3,
            [shaped(m, n)] + [shaped(*x.shape, dtype=x.dtype) for x in old], 2 * t * m * n * len(pairs),
        )
    return call(
        functools.partial(term_kernel, len(pairs), got is not None), "term", scalars, n // tile, ins, args, [out], [shaped(m, n)], 2 * t * m * n * len(pairs),
    )[0]


def stepped(g, w, m, v, new_w, new_m, new_v):
    one = 0.9 * m[0] + 0.1 * g
    two = 0.95 * v[0] + 0.05 * g * g
    wide = w[0].astype(F32)
    new_w[0] = (wide - 0.02 * (one * lax.rsqrt(two + 1e-8) + 0.1 * wide)).astype(BF16)
    new_m[0] = one
    new_v[0] = two


def last_term_kernel(pairs, _, *refs):
    total = refs[2 * pairs][...].astype(F32)
    for n in range(pairs):
        total = total + dot(refs[2 * n][...], refs[2 * n + 1][...], ((0,), (0,)))
    total = total.astype(BF16)
    refs[-4][...] = total
    stepped(total.astype(F32), *refs[2 * pairs + 1 : 2 * pairs + 4], *refs[-3:])


def adamw_kernel(terms, steps, s, *refs):
    w, m, v = refs[2 * terms : 2 * terms + 3] if steps else refs[terms : terms + 3]
    new_w, new_m, new_v = refs[-3:]

    def block(gs):
        g = gs[0][...].astype(F32)
        if terms == 2:
            g = (g + gs[1][...].astype(F32)).astype(BF16).astype(F32)
        stepped(g, w, m, v, new_w, new_m, new_v)

    if steps:
        pl.when(pl.program_id(0) < steps)(lambda: block(refs[:terms]))
        pl.when(pl.program_id(0) >= steps)(lambda: block(refs[terms : 2 * terms]))
    else:
        block(refs[:terms])


def adamw(terms, where, old, layer, tile, so_far, others=()):
    rows, cols = terms[0].shape
    steps = rows // tile

    def place(i, s):
        if not others:
            return (layer, s[0] * steps + i, s[1])
        later = (i >= steps).astype(jnp.int32)
        return (layer, jnp.where(later == 1, s[2] * steps + i - steps, s[0] * steps + i), jnp.where(later == 1, s[3], s[1]))

    block = pl.BlockSpec((1, tile, cols), place)
    g = [pl.BlockSpec((tile, cols), lambda i, s: (jnp.minimum(i, steps - 1), 0))] * len(terms)
    g += [pl.BlockSpec((tile, cols), lambda i, s: (jnp.maximum(i - steps, 0), 0))] * len(others)
    kept = list(so_far or ())
    scalars = jnp.stack([jnp.asarray(x, jnp.int32) for x in where])
    return call(
        functools.partial(adamw_kernel, len(terms), steps if others else 0), "adamw", scalars, steps * (2 if others else 1),
        g + [block] * 3 + [ANY] * len(kept), (*terms, *others, *old, *kept),
        [block] * 3, [shaped(*x.shape, dtype=x.dtype) for x in old], rows * cols * 4000, {len(g) + 4 + i: i for i in range(len(kept))},
    )


def after(x, *others):
    return lax.optimization_barrier((x, *others))[0]


def solution(mesh):
    def step(x, dy, *arrays):
        w, m, v = (arrays[i : i + 3] for i in (0, 3, 6))
        old = list(zip(w, m, v))
        h0, by1 = x[0], dy[0]
        _, d = h0.shape
        f = w[GATE].shape[-1]
        me = lax.axis_index("dp") % 2
        chip = lax.axis_index("dp") // 2
        sides = ((1 - me), me)
        zero = jnp.zeros((1,), jnp.int32)
        share, base = f // 2, chip * (f // 2 // TILE)

        def across(x):
            return lax.ppermute(x, "dp", ACROSS)

        def partner(x):
            return lax.ppermute(x, "dp", PARTNER)

        barrier = lax.optimization_barrier

        far_by1 = across(by1)
        a0, hidden0, gate0, up0 = forward(h0, w, 0, zero)
        h1 = barrier(h0 + dot(hidden0, w[DOWN][0], ((1,), (0,))).astype(BF16))
        far_h1 = across(h1)
        a1, hidden1, by_gate1, by_up1 = barrier(turn(h1, by1, w, 1, zero, f))
        by_a = dot(by_gate1, w[GATE][1], ((1,), (1,))).astype(BF16).astype(F32) + dot(by_up1, w[UP][1], ((1,), (1,))).astype(BF16).astype(F32)
        by_a, wide = by_a.astype(BF16).astype(F32), h1.astype(F32)
        scale = lax.rsqrt(jnp.mean(wide**2, -1, keepdims=True) + 1e-6)
        inner = jnp.sum(by_a * wide, -1, keepdims=True) / d
        by0 = barrier(by1 + (scale * by_a - wide * (scale**3 * inner)).astype(BF16))

        def left0(side, pair, size, tile, got=None):
            return term((side, 0), [pair], size, pair[1].shape[1], tile, got)

        sums, far, near = {}, {}, {}
        piece = f // 4
        theirs = [barrier(left0(sides[0] * 2, (hidden0, by0), piece, TILE))]
        got = [partner(theirs[0])]
        theirs.append(barrier(left0(sides[0] * 2 + 1, (after(hidden0, theirs[0]), by0), piece, TILE)))
        got.append(partner(theirs[1]))
        sums[DOWN] = [barrier(left0(sides[1] * 2, (after(hidden0, theirs[1]), by0), piece, TILE, got[0]))]
        far[DOWN] = [across(sums[DOWN][0])]
        near[DOWN] = [partner(sums[DOWN][0])]
        sums[DOWN].append(barrier(left0(sides[1] * 2 + 1, (after(hidden0, sums[DOWN][0]), by0), piece, TILE, got[1])))
        far[DOWN].append(across(sums[DOWN][1]))
        near[DOWN].append(partner(sums[DOWN][1]))
        by_gate0, by_up0 = barrier(back(after(by0, sums[DOWN][1]), w, gate0, up0, 0, zero))
        up_theirs = barrier(left0(sides[0], (a0, by_up0), d // 2, 512))
        up_got = partner(up_theirs)
        gate_theirs = barrier(left0(sides[0], (after(a0, up_theirs), by_gate0), d // 2, 512))
        gate_got = partner(gate_theirs)
        sums[UP] = barrier(left0(sides[1], (after(a0, gate_theirs), by_up0), d // 2, 512, up_got))
        far[UP] = across(sums[UP])
        near[UP] = partner(sums[UP])
        sums[GATE] = barrier(left0(sides[1], (after(a0, sums[UP]), by_gate0), d // 2, 512, gate_got))
        far[GATE] = across(sums[GATE])
        near[GATE] = partner(sums[GATE])

        far_h1, far_by1 = barrier((far_h1, far_by1, sums[GATE]))[:2]
        far_a1, far_hidden1, far_by_gate1, far_by_up1 = barrier(turn(far_h1, far_by1, w, 1, base[None].astype(jnp.int32), share))

        def left1(side, which, got=None, behind=None):
            if which == DOWN:
                pairs = [(hidden1, by1), (far_hidden1, far_by1)]
                places, size, n, tile = (chip * 2 + side, side, 0, 0), share // 2, d, TILE
            else:
                pairs = [(a1, (by_gate1, by_up1)[which]), (far_a1, (far_by_gate1, far_by_up1)[which])]
                places, size, n, tile = (side, side, base, 0), d // 2, share, TILE
            if behind is not None:
                pairs[0] = (after(pairs[0][0], behind), pairs[0][1])
            if got is None:
                return barrier(term(places, pairs, size, n, tile))
            corner = (chip * 2 + side, 0) if which == DOWN else (side, base)
            total, *new[which] = barrier(term(places + corner, pairs, size, n, tile, got, old[which], 1))
            return total

        new, theirs, own1 = [None] * 3, {}, {}
        theirs[DOWN] = left1(sides[0], DOWN)
        got = partner(theirs[DOWN])
        theirs[UP] = left1(sides[0], UP, None, theirs[DOWN])
        got_up = partner(theirs[UP])
        own1[DOWN] = left1(sides[1], DOWN, got, theirs[UP])
        far1 = {DOWN: across(own1[DOWN])}
        near1 = {DOWN: partner(own1[DOWN])}
        theirs[GATE] = left1(sides[0], GATE, None, own1[DOWN])
        got_gate = partner(theirs[GATE])
        own1[UP] = left1(sides[1], UP, got_up, theirs[GATE])
        far1[UP] = across(own1[UP])
        near1[UP] = partner(own1[UP])
        own1[GATE] = left1(sides[1], GATE, got_gate, own1[UP])
        far1[GATE] = across(own1[GATE])
        near1[GATE] = partner(own1[GATE])

        last = own1[GATE]

        def optimize(which, layer, terms, where, tile, others=()):
            nonlocal last
            both = barrier((*terms, *others, last))
            terms, others = both[: len(terms)], both[len(terms) : -1]
            new[which] = adamw(terms, where, old[which], layer, tile, new[which], others)
            last = new[which][0]

        arrived = {}

        def beside(which):
            here = after(far1[which], last)
            arrived[which] = (here, partner(here))

        def first_layer(which):
            if which == DOWN:
                here = list(barrier((*far[which], last))[:2])
                places = [(side * 2, 0, side * 2 + 1, 0) for side in (me, 1 - me)]
                optimize(which, 0, (sums[which][0], here[0]), places[0], 224, (sums[which][1], here[1]))
                there = [partner(here[n]) for n in range(2)]
                optimize(which, 0, (near[which][0], there[0]), places[1], 224, (near[which][1], there[1]))
                return
            here = after(far[which], last)
            optimize(which, 0, (sums[which], here), (me, 0), 192)
            there = partner(here)
            if which == GATE:
                beside(DOWN)
            optimize(which, 0, (near[which], there), (1 - me, 0), 192)

        def places(which, of_chip):
            return [(of_chip * 2 + side, 0) if which == DOWN else (side, of_chip) for side in (me, 1 - me)]

        first_layer(DOWN)
        for which in (DOWN, UP, GATE):
            optimize(which, 1, (near1[which],), places(which, chip)[1], 224 if which == DOWN else 192)
        first_layer(UP)
        first_layer(GATE)
        for which in (DOWN, UP):
            if which == DOWN:
                beside(UP)
            (here, there), (first, second) = arrived[which], places(which, 1 - chip)
            optimize(which, 1, (here,), first + second, 224 if which == DOWN else 192, (there,))
        first, second = places(GATE, 1 - chip)
        here = after(far1[GATE], last)
        optimize(GATE, 1, (here,), first, 192)
        optimize(GATE, 1, (partner(here),), second, 192)
        return tuple(new[i][which] for which in range(3) for i in range(3))

    mapped = jax.shard_map(
        step,
        mesh=mesh,
        in_specs=(P(("rep", "dp"), None, None),) * 2 + (P(None, None, None),) * 9,
        out_specs=(P("rep", None, None),) * 9,
        check_vma=False,
    )

    def traced(*args):
        shapes = [jax.ShapeDtypeStruct(x.shape, x.dtype) for x in args]
        jax.eval_shape(mapped, *shapes)
        return mapped(*args)

    return traced
```

time: 1890 us -> 1360 us (0.72)
  Pallas kernels: 0 us -> 721 us
  waiting for transfers between devices: 1080 us -> 500 us
  matrix products: 519 us -> 92.6 us
  other arithmetic: 248 us -> 17.9 us
    psum x1 -> x0, waiting for transfers between devices: 1080 us -> none  [step(): summed[number] = [lax.psum(by_w[name], 'dp') for name in NAMES]]
    pallas_call x0 -> x31, Pallas kernels: none -> 721 us  [call(): pl.pallas_call(kernel, grid_spec=pltpu.PrefetchScalarGridSpec(num_scalar_...]
    ppermute x0 -> x30, waiting for transfers between devices: none -> 500 us  [the longest x9 497 us: across(): return lax.ppermute(x, 'dp', ACROSS)]
    dot_general x15 -> x3, matrix products: 519 us -> 92.6 us  [dot(): return lax.dot_general(a, b, (dims, ((), ())), preferred_element_type=F32)]
    convert_element_type x2 -> x0, other arithmetic: 232 us -> none  [adamw(): return ((w - 0.02 * step).astype(jnp.bfloat16), m, v)]
  transfers between devices with their start and end apart: 1 -> 30, of which waited for: 1 -> 10; matrix products, arithmetic and copies ran while one was open for 0% -> 1% of each run, Pallas kernels for 0% -> 31%
where the time goes in v2:
time: 1360 us; the launch traced here: 1350 us
  Pallas kernels  721 us (53%)
  waiting for transfers between devices  500 us (37%)
  matrix products  92.6 us (7%)
  other arithmetic  17.9 us (1%)
  starting transfers between devices  16.2 us (1%)
    pallas_call x31, Pallas kernels, call(): pl.pallas_call(kernel, grid_spec=pltpu.PrefetchScalarGridSpec(num_scalar_...  721 us
    ppermute x9, waiting for transfers between devices, across(): return lax.ppermute(x, 'dp', ACROSS)  497 us
    dot_general x3, matrix products, dot(): return lax.dot_general(a, b, (dims, ((), ())), preferred_element_type=F32)  92.6 us
  transfers between devices with their start and end apart: 30, of which 10 were waited for; matrix products, arithmetic and copies ran while one was open for 1% of the time, Pallas kernels for 31%

profile of v2, /device:TPU:0, one launch (start us, length us, event | category | flops | bytes accessed | tf_op | source)
XLA Modules:
  0.0 1350.1 jit_solution(1105574874200090494)
XLA Ops:
  0.7 57.6 %shard_map.178 = (bf16[2048,1536]{1,0:T(8,128)(2,1)}, bf16[2048,3584]{1,0:T(8,128)(2,1)}, f32[2048,3584]{1,0:T(8,128)}, f32[2048,3584]{1,0:T(8,128)}) custom-call(s32[1]{0:T(128)} %constant.38.clone.1._, bf16[2048,1536]{1,0:T(8,128)(2,1)} %bitcast.45, bf16[2,1536,3584]{2,1,0:T(8,128)(2,1)} %refs_1_.9, bf16[2,1536,3584]{2,1,0:T(8,128)(2,1)} %refs_2_.19), custom_call_target="tpu_custom_call" | custom-call | flops 45097156608 | bytes 79691776 | tf_op jit(solution)/shard_map/pallas_call | solution.py:75
  58.2 30.3 %fusion.24.h = bf16[2048,1536]{1,0:T(8,128)(2,1)} fusion(bf16[2048,3584]{1,0:T(8,128)(2,1)} %get-tuple-element.128.refs_0_, bf16[2,3584,1536]{2,1,0:T(8,128)(2,1)} %refs_2_.18, bf16[1,2048,1536]{2,1,0:T(8,128)(2,1)} %param.11), kind=kOutput, calls=%fused_computation.21 | convolution fusion | flops 22554869760 | bytes 38273024 | tf_op jit(solution)/shard_map/dot_general | solution.py:22
  88.5 83.9 %shard_map.179 = (bf16[2048,1536]{1,0:T(8,128)(2,1)}, bf16[2048,3584]{1,0:T(8,128)(2,1)}, bf16[2048,3584]{1,0:T(8,128)(2,1)}, bf16[2048,3584]{1,0:T(8,128)(2,1)}) custom-call(s32[1]{0:T(128)} %constant.38.clone.1._, bf16[2048,1536]{1,0:T(8,128)(2,1)} %fusion.24.h, bf16[2048,1536]{1,0:T(8,128)(2,1)} %bitcast.41, bf16[2,1536,3584]{2,1,0:T(8,128)(2,1)} %refs_1_.9, ...), custom_call_target="tpu_custom_call" | custom-call | flops 67645734912 | bytes 50331648 | tf_op jit(solution)/shard_map/pallas_call | solution.py:75
  172.4 30.4 %fusion.16 = bf16[2048,1536]{1,0:T(8,128)(2,1)} fusion(bf16[2048,3584]{1,0:T(8,128)(2,1)} %get-tuple-element.124.refs_1_, bf16[2,1536,3584]{2,1,0:T(8,128)(2,1)} %refs_1_.9), kind=kOutput, calls=%fused_computation.19 | convolution fusion | flops 22551724032 | bytes 31981568 | tf_op jit(solution)/shard_map/dot_general | solution.py:22
  202.7 32.0 %fusion.2 = (f32[2048]{0:T(1024)S(1)}, f32[2048]{0:T(1024)S(1)}, bf16[2048,1536]{1,0:T(8,128)(2,1)}) fusion(bf16[2048,1536]{1,0:T(8,128)(2,1)} %fusion.24.h, bf16[2048,3584]{1,0:T(8,128)(2,1)} %get-tuple-element.125.refs_1_, bf16[2,1536,3584]{2,1,0:T(8,128)(2,1)} %refs_2_.19, bf16[2048,1536]{1,0:T(8,128)(2,1)} %fusion.16), kind=kOutput, calls=%fused_computation.6 | convolution fusion | flops 22583177216 | bytes 44580864 | tf_op jit(solution)/shard_map/dot_general | solution.py:22
  234.7 10.9 fusion.27.refs_1_.by
  245.6 0.7 pad_add_fusion
  246.3 11.4 shard_map.180
  257.7 0.8 collective-permute-start.2
  258.5 0.6 pad_add_fusion.2._
  259.2 11.4 shard_map.181
  270.6 0.6 pad_add_fusion.3._
  271.2 0.7 pad_add_fusion.4._
  271.9 0.7 pad_add_fusion.5
  272.5 12.0 shard_map.182.refs_0_
  284.6 11.9 shard_map.183.refs_2_
  296.4 45.0 %shard_map.184 = (bf16[2048,3584]{1,0:T(8,128)(2,1)}, bf16[2048,3584]{1,0:T(8,128)(2,1)}) custom-call(s32[1]{0:T(128)} %constant.38.clone.1._, bf16[2048,1536]{1,0:T(8,128)(2,1)} %fusion.27.refs_1_.by, bf16[2,3584,1536]{2,1,0:T(8,128)(2,1)} %refs_2_.18, f32[2048,3584]{1,0:T(8,128)} %get-tuple-element.130.gate, f32[2048,3584]{1,0:T(8,128)} %get-tuple-element.131.up), custom_call_target="tpu_custom_call" | custom-call | flops 22548578304 | bytes 29360128 | tf_op jit(solution)/shard_map/pallas_call | solution.py:75
  341.4 17.1 %shard_map.185 = bf16[768,3584]{1,0:T(8,128)(2,1)} custom-call(s32[2]{0:T(128)} %get-tuple-element.238._.s, bf16[2048,1536]{1,0:T(8,128)(2,1)} %get-tuple-element.136.refs_0_, bf16[2048,3584]{1,0:T(8,128)(2,1)} %get-tuple-element.132.refs_1_), custom_call_target="tpu_custom_call" | custom-call | flops 11274289152 | bytes 5505024 | tf_op jit(solution)/shard_map/pallas_call | solution.py:75
  358.9 17.1 %shard_map.186 = bf16[768,3584]{1,0:T(8,128)(2,1)} custom-call(s32[2]{0:T(128)} %get-tuple-element.238._.s, bf16[2048,1536]{1,0:T(8,128)(2,1)} %get-tuple-element.136.refs_0_, bf16[2048,3584]{1,0:T(8,128)(2,1)} %get-tuple-element.134.refs_1_), custom_call_target="tpu_custom_call" | custom-call | flops 11274289152 | bytes 5505024 | tf_op jit(solution)/shard_map/pallas_call | solution.py:75
  376.0 3.0 collective-permute-start
  379.0 0.6 pad_add_fusion.6._.s
  379.7 0.7 pad_add_fusion.10
  380.3 17.9 %shard_map.187.refs_0_ = bf16[768,3584]{1,0:T(8,128)(2,1)} custom-call(s32[2]{0:T(128)} %pad_add_fusion.6._.s, bf16[2048,1536]{1,0:T(8,128)(2,1)} %get-tuple-element.136.refs_0_, bf16[2048,3584]{1,0:T(8,128)(2,1)} %get-tuple-element.132.refs_1_, bf16[768,3584]{1,0:T(8,128)(2,1)} %collective-permute-done.4.refs_2_), custom_call_target="tpu_custom_call" | custom-call | flops 11274289152 | bytes 5505024 | tf_op jit(solution)/shard_map/pallas_call | solution.py:75
  398.3 18.0 %shard_map.188.refs_0_ = bf16[768,3584]{1,0:T(8,128)(2,1)} custom-call(s32[2]{0:T(128)} %pad_add_fusion.6._.s, bf16[2048,1536]{1,0:T(8,128)(2,1)} %get-tuple-element.136.refs_0_, bf16[2048,3584]{1,0:T(8,128)(2,1)} %get-tuple-element.134.refs_1_, bf16[768,3584]{1,0:T(8,128)(2,1)} %collective-permute-done.5.refs_2_), custom_call_target="tpu_custom_call" | custom-call | flops 11274289152 | bytes 5505024 | tf_op jit(solution)/shard_map/pallas_call | solution.py:75
  416.2 99.4 %collective-permute-done.h = bf16[2048,1536]{1,0:T(8,128)(2,1)} collective-permute-done((bf16[2048,1536]{1,0:T(8,128)(2,1)}, bf16[2048,1536]{1,0:T(8,128)(2,1)}, u32[]{:S(2)}, u32[]{:S(2)}) %collective-permute-start) | collective-permute-done | bytes 6291488 | tf_op jit(solution)/shard_map/ppermute | solution.py:238
  515.7 134.1 %collective-permute-done.1.by.refs_3_ = bf16[2048,1536]{1,0:T(8,128)(2,1)} collective-permute-done((bf16[2048,1536]{1,0:T(8,128)(2,1)}, bf16[2048,1536]{1,0:T(8,128)(2,1)}, u32[]{:S(2)}, u32[]{:S(2)}) %collective-permute-start.1) | collective-permute-done | bytes 6291488 | tf_op jit(solution)/shard_map/ppermute | solution.py:238
  649.8 47.5 %shard_map.189 = (bf16[2048,1536]{1,0:T(8,128)(2,1)}, bf16[2048,1792]{1,0:T(8,128)(2,1)}, bf16[2048,1792]{1,0:T(8,128)(2,1)}, bf16[2048,1792]{1,0:T(8,128)(2,1)}) custom-call(s32[1]{0:T(128)} %bitcast.3._, bf16[2048,1536]{1,0:T(8,128)(2,1)} %collective-permute-done.h, bf16[2048,1536]{1,0:T(8,128)(2,1)} %collective-permute-done.1.by.refs_3_, ...), custom_call_target="tpu_custom_call" | custom-call | flops 33822867456 | bytes 28311552 | tf_op jit(solution)/shard_map/pallas_call | solution.py:75
  697.3 18.1 %shard_map.190 = bf16[896,1536]{1,0:T(8,128)(2,1)} custom-call(s32[4]{0:T(128)} %get-tuple-element.241._, bf16[2048,3584]{1,0:T(8,128)(2,1)} %get-tuple-element.143.refs_0_, bf16[2048,1536]{1,0:T(8,128)(2,1)} %bitcast.43, bf16[2048,1792]{1,0:T(8,128)(2,1)} %get-tuple-element.139.refs_2_, bf16[2048,1536]{1,0:T(8,128)(2,1)} %collective-permute-done.1.by.refs_3_), custom_call_target="tpu_custom_call" | custom-call | flops 11274289152 | bytes 2752512 | tf_op jit(solution)/shard_map/pallas_call | solution.py:75
  715.4 0.6 stack.70._
  716.0 18.1 %shard_map.191 = bf16[768,1792]{1,0:T(8,128)(2,1)} custom-call(s32[4]{0:T(128)} %get-tuple-element.240._, bf16[2048,1536]{1,0:T(8,128)(2,1)} %get-tuple-element.149.refs_0_, bf16[2048,3584]{1,0:T(8,128)(2,1)} %get-tuple-element.125.refs_1_, bf16[2048,1536]{1,0:T(8,128)(2,1)} %get-tuple-element.141.refs_2_, bf16[2048,1792]{1,0:T(8,128)(2,1)} %get-tuple-element.142.refs_3_), custom_call_target="tpu_custom_call" | custom-call | flops 11274289152 | bytes 2752512 | tf_op jit(solution)/shard_map/pallas_call | solution.py:75
  734.6 24.6 %shard_map.192 = (bf16[896,1536]{1,0:T(8,128)(2,1)}, bf16[2,3584,1536]{2,1,0:T(8,128)(2,1)}, f32[2,3584,1536]{2,1,0:T(8,128)}, f32[2,3584,1536]{2,1,0:T(8,128)}) custom-call(s32[6]{0:T(128)} %stack.70._, bf16[2048,3584]{1,0:T(8,128)(2,1)} %get-tuple-element.143.refs_0_, bf16[2048,1536]{1,0:T(8,128)(2,1)} %bitcast.44, ...), custom_call_target="tpu_custom_call" | custom-call | flops 11274289152 | bytes 112852992 | tf_op jit(solution)/shard_map/pallas_call | solution.py:75
  759.2 18.5 %shard_map.193 = bf16[768,1792]{1,0:T(8,128)(2,1)} custom-call(s32[4]{0:T(128)} %get-tuple-element.240._, bf16[2048,1536]{1,0:T(8,128)(2,1)} %get-tuple-element.149.refs_0_, bf16[2048,3584]{1,0:T(8,128)(2,1)} %get-tuple-element.124.refs_1_, bf16[2048,1536]{1,0:T(8,128)(2,1)} %get-tuple-element.141.refs_2_, bf16[2048,1792]{1,0:T(8,128)(2,1)} %get-tuple-element.146.refs_3_), custom_call_target="tpu_custom_call" | custom-call | flops 11274289152 | bytes 2752512 | tf_op jit(solution)/shard_map/pallas_call | solution.py:75
  777.7 1.7 collective-permute-start.20
  779.7 0.6 stack.67._
  780.9 25.0 %shard_map.194 = (bf16[768,1792]{1,0:T(8,128)(2,1)}, bf16[2,1536,3584]{2,1,0:T(8,128)(2,1)}, f32[2,1536,3584]{2,1,0:T(8,128)}, f32[2,1536,3584]{2,1,0:T(8,128)}) custom-call(s32[6]{0:T(128)} %stack.67._, bf16[2048,1536]{1,0:T(8,128)(2,1)} %get-tuple-element.149.refs_0_, bf16[2048,3584]{1,0:T(8,128)(2,1)} %get-tuple-element.125.refs_1_, ...), custom_call_target="tpu_custom_call" | custom-call | flops 11274289152 | bytes 112852992 | tf_op jit(solution)/shard_map/pallas_call | solution.py:75
  805.9 25.0 %shard_map.195 = (bf16[768,1792]{1,0:T(8,128)(2,1)}, bf16[2,1536,3584]{2,1,0:T(8,128)(2,1)}, f32[2,1536,3584]{2,1,0:T(8,128)}, f32[2,1536,3584]{2,1,0:T(8,128)}) custom-call(s32[6]{0:T(128)} %stack.67._, bf16[2048,1536]{1,0:T(8,128)(2,1)} %get-tuple-element.149.refs_0_, bf16[2048,3584]{1,0:T(8,128)(2,1)} %get-tuple-element.124.refs_1_, ...), custom_call_target="tpu_custom_call" | custom-call | flops 11274289152 | bytes 112852992 | tf_op jit(solution)/shard_map/pallas_call | solution.py:75
  830.9 9.7 collective-permute-done.20.refs_3_
  840.6 58.5 %collective-permute-done.19.refs_1_ = bf16[896,1536]{1,0:T(8,128)(2,1)} collective-permute-done((bf16[896,1536]{1,0:T(8,128)(2,1)}, bf16[896,1536]{1,0:T(8,128)(2,1)}, u32[]{:S(2)}, u32[]{:S(2)}) %collective-permute-start.19) | collective-permute-done | bytes 2752544 | tf_op jit(solution)/shard_map/ppermute | solution.py:238
  899.1 1.7 collective-permute-start.14
  901.6 2.9 collective-permute-done.21.refs_1_
  905.2 0.7 pad_add_fusion.7
  905.9 24.4 %shard_map.196 = (bf16[2,3584,1536]{2,1,0:T(8,128)(2,1)}, f32[2,3584,1536]{2,1,0:T(8,128)}, f32[2,3584,1536]{2,1,0:T(8,128)}) custom-call(s32[4]{0:T(128)} %get-tuple-element.245.s, bf16[896,1536]{1,0:T(8,128)(2,1)} %shard_map.182.refs_0_, ...), custom_call_target="tpu_custom_call", output_to_operand_aliasing={{0}: (8, {}), {1}: (9, {}), {2}: (10, {})} | custom-call | flops 5505024000 | bytes 110100480 | tf_op jit(solution)/shard_map/pallas_call | solution.py:75
  930.7 24.4 %shard_map.197 = (bf16[2,3584,1536]{2,1,0:T(8,128)(2,1)}, f32[2,3584,1536]{2,1,0:T(8,128)}, f32[2,3584,1536]{2,1,0:T(8,128)}) custom-call(s32[4]{0:T(128)} %pad_add_fusion.9.s, bf16[896,1536]{1,0:T(8,128)(2,1)} %collective-permute-done.18.refs_0_, ...), custom_call_target="tpu_custom_call", output_to_operand_aliasing={{0}: (8, {}), {1}: (9, {}), {2}: (10, {})} | custom-call | flops 5505024000 | bytes 110100480 | tf_op jit(solution)/shard_map/pallas_call | solution.py:75
  955.2 11.9 shard_map.198
  967.1 11.8 shard_map.199
  978.9 11.8 shard_map.200
  990.7 29.8 %collective-permute-done.14.refs_1_ = bf16[768,3584]{1,0:T(8,128)(2,1)} collective-permute-done((bf16[768,3584]{1,0:T(8,128)(2,1)}, bf16[768,3584]{1,0:T(8,128)(2,1)}, u32[]{:S(2)}, u32[]{:S(2)}) %collective-permute-start.14) | collective-permute-done | bytes 5505056 | tf_op jit(solution)/shard_map/ppermute | solution.py:238
  1020.5 1.7 collective-permute-start.12
  1022.5 21.9 %shard_map.201 = (bf16[2,1536,3584]{2,1,0:T(8,128)(2,1)}, f32[2,1536,3584]{2,1,0:T(8,128)}, f32[2,1536,3584]{2,1,0:T(8,128)}) custom-call(s32[2]{0:T(128)} %pad_add_fusion.6._.s, bf16[768,3584]{1,0:T(8,128)(2,1)} %shard_map.187.refs_0_, ...), custom_call_target="tpu_custom_call", output_to_operand_aliasing={{0}: (6, {}), {1}: (7, {}), {2}: (8, {})} | custom-call | flops 11010048000 | bytes 110100480 | tf_op jit(solution)/shard_map/pallas_call | solution.py:75
  1044.4 22.0 %shard_map.202 = (bf16[2,1536,3584]{2,1,0:T(8,128)(2,1)}, f32[2,1536,3584]{2,1,0:T(8,128)}, f32[2,1536,3584]{2,1,0:T(8,128)}) custom-call(s32[2]{0:T(128)} %get-tuple-element.238._.s, bf16[768,3584]{1,0:T(8,128)(2,1)} %collective-permute-done.13.refs_0_, ...), custom_call_target="tpu_custom_call", output_to_operand_aliasing={{0}: (6, {}), {1}: (7, {}), {2}: (8, {})} | custom-call | flops 11010048000 | bytes 110100480 | tf_op jit(solution)/shard_map/pallas_call | solution.py:75
  1066.4 75.5 %collective-permute-done.12.refs_1_ = bf16[768,3584]{1,0:T(8,128)(2,1)} collective-permute-done((bf16[768,3584]{1,0:T(8,128)(2,1)}, bf16[768,3584]{1,0:T(8,128)(2,1)}, u32[]{:S(2)}, u32[]{:S(2)}) %collective-permute-start.12) | collective-permute-done | bytes 5505056 | tf_op jit(solution)/shard_map/ppermute | solution.py:238
  1141.9 1.7 collective-permute-start.27
  1143.9 21.9 %shard_map.203 = (bf16[2,1536,3584]{2,1,0:T(8,128)(2,1)}, f32[2,1536,3584]{2,1,0:T(8,128)}, f32[2,1536,3584]{2,1,0:T(8,128)}) custom-call(s32[2]{0:T(128)} %pad_add_fusion.6._.s, bf16[768,3584]{1,0:T(8,128)(2,1)} %shard_map.188.refs_0_, ...), custom_call_target="tpu_custom_call", output_to_operand_aliasing={{0}: (6, {}), {1}: (7, {}), {2}: (8, {})} | custom-call | flops 11010048000 | bytes 110100480 | tf_op jit(solution)/shard_map/pallas_call | solution.py:75
  1165.9 38.9 %collective-permute-done.27.refs_0_ = bf16[896,1536]{1,0:T(8,128)(2,1)} collective-permute-done((bf16[896,1536]{1,0:T(8,128)(2,1)}, bf16[896,1536]{1,0:T(8,128)(2,1)}, u32[]{:S(2)}, u32[]{:S(2)}) %collective-permute-start.27) | collective-permute-done | bytes 2752544 | tf_op jit(solution)/shard_map/ppermute | solution.py:238
  1204.8 22.2 %shard_map.204 = (bf16[2,1536,3584]{2,1,0:T(8,128)(2,1)}, f32[2,1536,3584]{2,1,0:T(8,128)}, f32[2,1536,3584]{2,1,0:T(8,128)}) custom-call(s32[2]{0:T(128)} %get-tuple-element.238._.s, bf16[768,3584]{1,0:T(8,128)(2,1)} %collective-permute-done.11.refs_0_, ...), custom_call_target="tpu_custom_call", output_to_operand_aliasing={{0}: (6, {}), {1}: (7, {}), {2}: (8, {})} | custom-call | flops 11010048000 | bytes 110100480 | tf_op jit(solution)/shard_map/pallas_call | solution.py:75
  1226.9 36.3 %collective-permute-done.10.refs_0_ = bf16[768,1792]{1,0:T(8,128)(2,1)} collective-permute-done((bf16[768,1792]{1,0:T(8,128)(2,1)}, bf16[768,1792]{1,0:T(8,128)(2,1)}, u32[]{:S(2)}, u32[]{:S(2)}) %collective-permute-start.10) | collective-permute-done | bytes 2752544 | tf_op jit(solution)/shard_map/ppermute | solution.py:238
  1263.3 1.7 collective-permute-start.9
  1265.0 0.6 pad_add_fusion.15.s
  1265.6 22.9 %shard_map.205 = (bf16[2,3584,1536]{2,1,0:T(8,128)(2,1)}, f32[2,3584,1536]{2,1,0:T(8,128)}, f32[2,3584,1536]{2,1,0:T(8,128)}) custom-call(s32[4]{0:T(128)} %get-tuple-element.244.s, bf16[896,1536]{1,0:T(8,128)(2,1)} %collective-permute-done.27.refs_0_, ...), custom_call_target="tpu_custom_call", output_to_operand_aliasing={{0}: (6, {}), {1}: (7, {}), {2}: (8, {})} | custom-call | flops 5505024000 | bytes 110100480 | tf_op jit(solution)/shard_map/pallas_call | solution.py:75
  1288.5 22.9 %shard_map.206 = (bf16[2,1536,3584]{2,1,0:T(8,128)(2,1)}, f32[2,1536,3584]{2,1,0:T(8,128)}, f32[2,1536,3584]{2,1,0:T(8,128)}) custom-call(s32[4]{0:T(128)} %pad_add_fusion.15.s, bf16[768,1792]{1,0:T(8,128)(2,1)} %collective-permute-done.10.refs_0_, ...), custom_call_target="tpu_custom_call", output_to_operand_aliasing={{0}: (6, {}), {1}: (7, {}), {2}: (8, {})} | custom-call | flops 5505024000 | bytes 110100480 | tf_op jit(solution)/shard_map/pallas_call | solution.py:75
  1311.4 14.3 %collective-permute-done.9.refs_0_ = bf16[768,1792]{1,0:T(8,128)(2,1)} collective-permute-done((bf16[768,1792]{1,0:T(8,128)(2,1)}, bf16[768,1792]{1,0:T(8,128)(2,1)}, u32[]{:S(2)}, u32[]{:S(2)}) %collective-permute-start.9) | collective-permute-done | bytes 2752544 | tf_op jit(solution)/shard_map/ppermute | solution.py:238
  1325.7 0.6 pad_add_fusion.17
  1326.3 11.8 shard_map.207
  1338.1 11.8 shard_map.208
  (46 shorter events, 4.3 us)
Async XLA Ops:
  257.7 14.9 %collective-permute-start.2 = (bf16[896,1536]{1,0:T(8,128)(2,1)}, bf16[896,1536]{1,0:T(8,128)(2,1)}, u32[]{:S(2)}, u32[]{:S(2)}) collective-permute-start(bf16[896,1536]{1,0:T(8,128)(2,1)} %shard_map.180), channel_id=1, source_target_pairs={{0,1},{1,0},{2,3},{3,2},{4,5},{5,4},{6,7},{7,6}} | collective-permute-start | bytes 8257544 | tf_op jit(solution)/shard_map/ppermute | solution.py:241
  270.6 14.0 %collective-permute-start.3 = (bf16[896,1536]{1,0:T(8,128)(2,1)}, bf16[896,1536]{1,0:T(8,128)(2,1)}, u32[]{:S(2)}, u32[]{:S(2)}) collective-permute-start(bf16[896,1536]{1,0:T(8,128)(2,1)} %shard_map.181), channel_id=1, source_target_pairs={{0,1},{1,0},{2,3},{3,2},{4,5},{5,4},{6,7},{7,6}} | collective-permute-start | bytes 8257544 | tf_op jit(solution)/shard_map/ppermute | solution.py:241
  358.4 21.9 %collective-permute-start.4 = (bf16[768,3584]{1,0:T(8,128)(2,1)}, bf16[768,3584]{1,0:T(8,128)(2,1)}, u32[]{:S(2)}, u32[]{:S(2)}) collective-permute-start(bf16[768,3584]{1,0:T(8,128)(2,1)} %shard_map.185), channel_id=1, source_target_pairs={{0,1},{1,0},{2,3},{3,2},{4,5},{5,4},{6,7},{7,6}} | collective-permute-start | bytes 16515080 | tf_op jit(solution)/shard_map/ppermute | solution.py:241
  376.0 22.2 %collective-permute-start.5 = (bf16[768,3584]{1,0:T(8,128)(2,1)}, bf16[768,3584]{1,0:T(8,128)(2,1)}, u32[]{:S(2)}, u32[]{:S(2)}) collective-permute-start(bf16[768,3584]{1,0:T(8,128)(2,1)} %shard_map.186), channel_id=1, source_target_pairs={{0,1},{1,0},{2,3},{3,2},{4,5},{5,4},{6,7},{7,6}} | collective-permute-start | bytes 16515080 | tf_op jit(solution)/shard_map/ppermute | solution.py:241
  376.0 139.7 %collective-permute-start = (bf16[2048,1536]{1,0:T(8,128)(2,1)}, bf16[2048,1536]{1,0:T(8,128)(2,1)}, u32[]{:S(2)}, u32[]{:S(2)}) collective-permute-start(bf16[2048,1536]{1,0:T(8,128)(2,1)} %fusion.24.h), channel_id=1, source_target_pairs={{0,2},{2,0},{1,3},{3,1},{4,6},{6,4},{5,7},{7,5}} | collective-permute-start | bytes 18874376 | tf_op jit(solution)/shard_map/ppermute | solution.py:238
  379.0 270.8 %collective-permute-start.1 = (bf16[2048,1536]{1,0:T(8,128)(2,1)}, bf16[2048,1536]{1,0:T(8,128)(2,1)}, u32[]{:S(2)}, u32[]{:S(2)}) collective-permute-start(bf16[2048,1536]{1,0:T(8,128)(2,1)} %bitcast.42), channel_id=1, source_target_pairs={{0,2},{2,0},{1,3},{3,1},{4,6},{6,4},{5,7},{7,5}} | collective-permute-start | bytes 18874376 | tf_op jit(solution)/shard_map/ppermute | solution.py:238
  715.4 19.2 %collective-permute-start.6 = (bf16[896,1536]{1,0:T(8,128)(2,1)}, bf16[896,1536]{1,0:T(8,128)(2,1)}, u32[]{:S(2)}, u32[]{:S(2)}) collective-permute-start(bf16[896,1536]{1,0:T(8,128)(2,1)} %shard_map.190), channel_id=1, source_target_pairs={{0,1},{1,0},{2,3},{3,2},{4,5},{5,4},{6,7},{7,6}} | collective-permute-start | bytes 8257544 | tf_op jit(solution)/shard_map/ppermute | solution.py:241
  734.1 46.3 %collective-permute-start.7 = (bf16[768,1792]{1,0:T(8,128)(2,1)}, bf16[768,1792]{1,0:T(8,128)(2,1)}, u32[]{:S(2)}, u32[]{:S(2)}) collective-permute-start(bf16[768,1792]{1,0:T(8,128)(2,1)} %shard_map.191), channel_id=1, source_target_pairs={{0,1},{1,0},{2,3},{3,2},{4,5},{5,4},{6,7},{7,6}} | collective-permute-start | bytes 8257544 | tf_op jit(solution)/shard_map/ppermute | solution.py:241
  777.7 28.2 %collective-permute-start.8 = (bf16[768,1792]{1,0:T(8,128)(2,1)}, bf16[768,1792]{1,0:T(8,128)(2,1)}, u32[]{:S(2)}, u32[]{:S(2)}) collective-permute-start(bf16[768,1792]{1,0:T(8,128)(2,1)} %shard_map.193), channel_id=1, source_target_pairs={{0,1},{1,0},{2,3},{3,2},{4,5},{5,4},{6,7},{7,6}} | collective-permute-start | bytes 8257544 | tf_op jit(solution)/shard_map/ppermute | solution.py:241
  777.7 62.9 %collective-permute-start.20 = (bf16[896,1536]{1,0:T(8,128)(2,1)}, bf16[896,1536]{1,0:T(8,128)(2,1)}, u32[]{:S(2)}, u32[]{:S(2)}) collective-permute-start(bf16[896,1536]{1,0:T(8,128)(2,1)} %shard_map.183.refs_2_), channel_id=1, source_target_pairs={{0,2},{2,0},{1,3},{3,1},{4,6},{6,4},{5,7},{7,5}} | collective-permute-start | bytes 8257544 | tf_op jit(solution)/shard_map/ppermute | solution.py:238
  779.5 119.6 %collective-permute-start.19 = (bf16[896,1536]{1,0:T(8,128)(2,1)}, bf16[896,1536]{1,0:T(8,128)(2,1)}, u32[]{:S(2)}, u32[]{:S(2)}) collective-permute-start(bf16[896,1536]{1,0:T(8,128)(2,1)} %shard_map.182.refs_0_), channel_id=1, source_target_pairs={{0,2},{2,0},{1,3},{3,1},{4,6},{6,4},{5,7},{7,5}} | collective-permute-start | bytes 8257544 | tf_op jit(solution)/shard_map/ppermute | solution.py:238
  780.4 120.7 %collective-permute-start.22 = (bf16[896,1536]{1,0:T(8,128)(2,1)}, bf16[896,1536]{1,0:T(8,128)(2,1)}, u32[]{:S(2)}, u32[]{:S(2)}) collective-permute-start(bf16[896,1536]{1,0:T(8,128)(2,1)} %shard_map.183.refs_2_), channel_id=1, source_target_pairs={{0,1},{1,0},{2,3},{3,2},{4,5},{5,4},{6,7},{7,6}} | collective-permute-start | bytes 8257544 | tf_op jit(solution)/shard_map/ppermute | solution.py:241
  780.4 121.0 %collective-permute-start.18 = (bf16[896,1536]{1,0:T(8,128)(2,1)}, bf16[896,1536]{1,0:T(8,128)(2,1)}, u32[]{:S(2)}, u32[]{:S(2)}) collective-permute-start(bf16[896,1536]{1,0:T(8,128)(2,1)} %shard_map.182.refs_0_), channel_id=1, source_target_pairs={{0,1},{1,0},{2,3},{3,2},{4,5},{5,4},{6,7},{7,6}} | collective-permute-start | bytes 8257544 | tf_op jit(solution)/shard_map/ppermute | solution.py:241
  899.1 5.4 collective-permute-start.21
  899.1 121.4 %collective-permute-start.14 = (bf16[768,3584]{1,0:T(8,128)(2,1)}, bf16[768,3584]{1,0:T(8,128)(2,1)}, u32[]{:S(2)}, u32[]{:S(2)}) collective-permute-start(bf16[768,3584]{1,0:T(8,128)(2,1)} %shard_map.187.refs_0_), channel_id=1, source_target_pairs={{0,2},{2,0},{1,3},{3,1},{4,6},{6,4},{5,7},{7,5}} | collective-permute-start | bytes 16515080 | tf_op jit(solution)/shard_map/ppermute | solution.py:238
  900.9 29.5 %collective-permute-start.23 = (bf16[896,1536]{1,0:T(8,128)(2,1)}, bf16[896,1536]{1,0:T(8,128)(2,1)}, u32[]{:S(2)}, u32[]{:S(2)}) collective-permute-start(bf16[896,1536]{1,0:T(8,128)(2,1)} %collective-permute-done.20.refs_3_), channel_id=1, source_target_pairs={{0,1},{1,0},{2,3},{3,2},{4,5},{5,4},{6,7},{7,6}} | collective-permute-start | bytes 8257544 | tf_op jit(solution)/shard_map/ppermute | solution.py:241
  901.1 54.1 %collective-permute-start.17 = (bf16[896,1536]{1,0:T(8,128)(2,1)}, bf16[896,1536]{1,0:T(8,128)(2,1)}, u32[]{:S(2)}, u32[]{:S(2)}) collective-permute-start(bf16[896,1536]{1,0:T(8,128)(2,1)} %get-tuple-element.144), channel_id=1, source_target_pairs={{0,1},{1,0},{2,3},{3,2},{4,5},{5,4},{6,7},{7,6}} | collective-permute-start | bytes 8257544 | tf_op jit(solution)/shard_map/ppermute | solution.py:241
  901.4 65.7 %collective-permute-start.16 = (bf16[768,1792]{1,0:T(8,128)(2,1)}, bf16[768,1792]{1,0:T(8,128)(2,1)}, u32[]{:S(2)}, u32[]{:S(2)}) collective-permute-start(bf16[768,1792]{1,0:T(8,128)(2,1)} %get-tuple-element.148), channel_id=1, source_target_pairs={{0,1},{1,0},{2,3},{3,2},{4,5},{5,4},{6,7},{7,6}} | collective-permute-start | bytes 8257544 | tf_op jit(solution)/shard_map/ppermute | solution.py:241
  904.5 74.3 %collective-permute-start.15 = (bf16[768,1792]{1,0:T(8,128)(2,1)}, bf16[768,1792]{1,0:T(8,128)(2,1)}, u32[]{:S(2)}, u32[]{:S(2)}) collective-permute-start(bf16[768,1792]{1,0:T(8,128)(2,1)} %get-tuple-element.150), channel_id=1, source_target_pairs={{0,1},{1,0},{2,3},{3,2},{4,5},{5,4},{6,7},{7,6}} | collective-permute-start | bytes 8257544 | tf_op jit(solution)/shard_map/ppermute | solution.py:241
  930.3 114.1 %collective-permute-start.13 = (bf16[768,3584]{1,0:T(8,128)(2,1)}, bf16[768,3584]{1,0:T(8,128)(2,1)}, u32[]{:S(2)}, u32[]{:S(2)}) collective-permute-start(bf16[768,3584]{1,0:T(8,128)(2,1)} %shard_map.187.refs_0_), channel_id=1, source_target_pairs={{0,1},{1,0},{2,3},{3,2},{4,5},{5,4},{6,7},{7,6}} | collective-permute-start | bytes 16515080 | tf_op jit(solution)/shard_map/ppermute | solution.py:241
  1020.5 23.9 %collective-permute-start.24 = (bf16[768,3584]{1,0:T(8,128)(2,1)}, bf16[768,3584]{1,0:T(8,128)(2,1)}, u32[]{:S(2)}, u32[]{:S(2)}) collective-permute-start(bf16[768,3584]{1,0:T(8,128)(2,1)} %collective-permute-done.14.refs_1_), channel_id=1, source_target_pairs={{0,1},{1,0},{2,3},{3,2},{4,5},{5,4},{6,7},{7,6}} | collective-permute-start | bytes 16515080 | tf_op jit(solution)/shard_map/ppermute | solution.py:241
  1020.5 121.4 %collective-permute-start.12 = (bf16[768,3584]{1,0:T(8,128)(2,1)}, bf16[768,3584]{1,0:T(8,128)(2,1)}, u32[]{:S(2)}, u32[]{:S(2)}) collective-permute-start(bf16[768,3584]{1,0:T(8,128)(2,1)} %shard_map.188.refs_0_), channel_id=1, source_target_pairs={{0,2},{2,0},{1,3},{3,1},{4,6},{6,4},{5,7},{7,5}} | collective-permute-start | bytes 16515080 | tf_op jit(solution)/shard_map/ppermute | solution.py:238
  1022.2 182.5 %collective-permute-start.11 = (bf16[768,3584]{1,0:T(8,128)(2,1)}, bf16[768,3584]{1,0:T(8,128)(2,1)}, u32[]{:S(2)}, u32[]{:S(2)}) collective-permute-start(bf16[768,3584]{1,0:T(8,128)(2,1)} %shard_map.188.refs_0_), channel_id=1, source_target_pairs={{0,1},{1,0},{2,3},{3,2},{4,5},{5,4},{6,7},{7,6}} | collective-permute-start | bytes 16515080 | tf_op jit(solution)/shard_map/ppermute | solution.py:241
  1141.9 62.9 %collective-permute-start.25 = (bf16[768,3584]{1,0:T(8,128)(2,1)}, bf16[768,3584]{1,0:T(8,128)(2,1)}, u32[]{:S(2)}, u32[]{:S(2)}) collective-permute-start(bf16[768,3584]{1,0:T(8,128)(2,1)} %collective-permute-done.12.refs_1_), channel_id=1, source_target_pairs={{0,1},{1,0},{2,3},{3,2},{4,5},{5,4},{6,7},{7,6}} | collective-permute-start | bytes 16515080 | tf_op jit(solution)/shard_map/ppermute | solution.py:241
  1141.9 62.9 %collective-permute-start.27 = (bf16[896,1536]{1,0:T(8,128)(2,1)}, bf16[896,1536]{1,0:T(8,128)(2,1)}, u32[]{:S(2)}, u32[]{:S(2)}) collective-permute-start(bf16[896,1536]{1,0:T(8,128)(2,1)} %get-tuple-element.144), channel_id=1, source_target_pairs={{0,2},{2,0},{1,3},{3,1},{4,6},{6,4},{5,7},{7,5}} | collective-permute-start | bytes 8257544 | tf_op jit(solution)/shard_map/ppermute | solution.py:238
  1143.6 119.6 %collective-permute-start.10 = (bf16[768,1792]{1,0:T(8,128)(2,1)}, bf16[768,1792]{1,0:T(8,128)(2,1)}, u32[]{:S(2)}, u32[]{:S(2)}) collective-permute-start(bf16[768,1792]{1,0:T(8,128)(2,1)} %get-tuple-element.148), channel_id=1, source_target_pairs={{0,2},{2,0},{1,3},{3,1},{4,6},{6,4},{5,7},{7,5}} | collective-permute-start | bytes 8257544 | tf_op jit(solution)/shard_map/ppermute | solution.py:238
  1204.8 60.9 %collective-permute-start.28 = (bf16[896,1536]{1,0:T(8,128)(2,1)}, bf16[896,1536]{1,0:T(8,128)(2,1)}, u32[]{:S(2)}, u32[]{:S(2)}) collective-permute-start(bf16[896,1536]{1,0:T(8,128)(2,1)} %collective-permute-done.27.refs_0_), channel_id=1, source_target_pairs={{0,1},{1,0},{2,3},{3,2},{4,5},{5,4},{6,7},{7,6}} | collective-permute-start | bytes 8257544 | tf_op jit(solution)/shard_map/ppermute | solution.py:241
  1263.3 25.2 %collective-permute-start.26 = (bf16[768,1792]{1,0:T(8,128)(2,1)}, bf16[768,1792]{1,0:T(8,128)(2,1)}, u32[]{:S(2)}, u32[]{:S(2)}) collective-permute-start(bf16[768,1792]{1,0:T(8,128)(2,1)} %collective-permute-done.10.refs_0_), channel_id=1, source_target_pairs={{0,1},{1,0},{2,3},{3,2},{4,5},{5,4},{6,7},{7,6}} | collective-permute-start | bytes 8257544 | tf_op jit(solution)/shard_map/ppermute | solution.py:241
  1263.3 62.4 %collective-permute-start.9 = (bf16[768,1792]{1,0:T(8,128)(2,1)}, bf16[768,1792]{1,0:T(8,128)(2,1)}, u32[]{:S(2)}, u32[]{:S(2)}) collective-permute-start(bf16[768,1792]{1,0:T(8,128)(2,1)} %get-tuple-element.150), channel_id=1, source_target_pairs={{0,2},{2,0},{1,3},{3,1},{4,6},{6,4},{5,7},{7,5}} | collective-permute-start | bytes 8257544 | tf_op jit(solution)/shard_map/ppermute | solution.py:238
  1325.7 12.4 collective-permute-start.29

commit v3 on v2

--- a/solution.py
+++ b/solution.py
@@ -70,11 +70,11 @@
         by_gate[rows], by_up[rows], _ = backward(dot(by[rows], w_down[0], ((1,), (1,))), gate[rows], up[rows])
 
 
-def call(kernel, name, scalars, tiles, ins, args, outs, shapes, flops, aliases={}):
+def call(kernel, name, scalars, tiles, ins, args, outs, shapes, flops, aliases={}, scratch=()):
     moved = sum(x.size * x.dtype.itemsize for x in shapes)
     return pl.pallas_call(
         kernel,
-        grid_spec=pltpu.PrefetchScalarGridSpec(num_scalar_prefetch=1, grid=(tiles,), in_specs=ins, out_specs=outs),
+        grid_spec=pltpu.PrefetchScalarGridSpec(num_scalar_prefetch=1, grid=(tiles,), in_specs=ins, out_specs=outs, scratch_shapes=scratch),
         out_shape=shapes,
         input_output_aliases=aliases,
         cost_estimate=cost(flops, moved),
@@ -137,7 +137,7 @@
     out[...] = total.astype(BF16)
 
 
-def term(where, pairs, m, n, tile, got=None, old=None, layer=None):
+def term(where, pairs, m, n, tile, got=None, old=None, layer=None, so_far=None, beside=None):
     t = pairs[0][0].shape[0]
     ins, args = [], []
     for i, (left, right) in enumerate(pairs):
@@ -149,24 +149,37 @@
         ins.append(out)
         args.append(got)
     scalars = jnp.stack([jnp.asarray(x, jnp.int32) for x in where])
+    kept = list(so_far or ())
     if old is not None:
         block = pl.BlockSpec((1, m, tile), lambda j, s: (layer, s[2 * len(pairs)], s[2 * len(pairs) + 1] + j))
         return call(
-            functools.partial(last_term_kernel, len(pairs)), "term", scalars, n // tile, ins + [block] * 3, args + list(old), [out] + [block] * 3,
-            [shaped(m, n)] + [shaped(*x.shape, dtype=x.dtype) for x in old], 2 * t * m * n * len(pairs),
+            functools.partial(last_term_kernel, len(pairs)), "term", scalars, n // tile, ins + [block] * 3 + [ANY] * len(kept), args + list(old) + kept,
+            [out] + [block] * 3, [shaped(m, n)] + [shaped(*x.shape, dtype=x.dtype) for x in old], 2 * t * m * n * len(pairs),
+            {2 * len(pairs) + 5 + i: 1 + i for i in range(len(kept))},
+        )
+    if beside is not None:
+        terms, old, layer = beside
+        rows, cols = terms[0].shape
+        rows //= n // tile
+        block = pl.BlockSpec((1, rows, cols), lambda j, s: (layer, s[2 * len(pairs)] * (n // tile) + j, 0))
+        return call(
+            functools.partial(beside_kernel, len(pairs)), "term", scalars, n // tile,
+            ins + [pl.BlockSpec((rows, cols), lambda j, s: (j, 0))] * 2 + [block] * 3 + [ANY] * len(kept), args + list(terms) + list(old) + kept,
+            [out] + [block] * 3, [shaped(m, n)] + [shaped(*x.shape, dtype=x.dtype) for x in old], 2 * t * m * n * len(pairs),
+            {2 * len(pairs) + 6 + i: 1 + i for i in range(len(kept))},
         )
     return call(
         functools.partial(term_kernel, len(pairs), got is not None), "term", scalars, n // tile, ins, args, [out], [shaped(m, n)], 2 * t * m * n * len(pairs),
     )[0]
 
 
-def stepped(g, w, m, v, new_w, new_m, new_v):
-    one = 0.9 * m[0] + 0.1 * g
-    two = 0.95 * v[0] + 0.05 * g * g
-    wide = w[0].astype(F32)
-    new_w[0] = (wide - 0.02 * (one * lax.rsqrt(two + 1e-8) + 0.1 * wide)).astype(BF16)
-    new_m[0] = one
-    new_v[0] = two
+def stepped(g, w, m, v, new_w, new_m, new_v, rows=slice(None)):
+    one = 0.9 * m[0, rows] + 0.1 * g
+    two = 0.95 * v[0, rows] + 0.05 * g * g
+    wide = w[0, rows].astype(F32)
+    new_w[0, rows] = (wide - 0.02 * (one * lax.rsqrt(two + 1e-8) + 0.1 * wide)).astype(BF16)
+    new_m[0, rows] = one
+    new_v[0, rows] = two
 
 
 def last_term_kernel(pairs, _, *refs):
@@ -178,15 +191,28 @@
     stepped(total.astype(F32), *refs[2 * pairs + 1 : 2 * pairs + 4], *refs[-3:])
 
 
+def beside_kernel(pairs, _, *refs):
+    total = None
+    for n in range(pairs):
+        part = dot(refs[2 * n][...], refs[2 * n + 1][...], ((0,), (0,)))
+        total = part if total is None else total + part
+    refs[-4][...] = total.astype(BF16)
+    g = (refs[2 * pairs][...].astype(F32) + refs[2 * pairs + 1][...].astype(F32)).astype(BF16).astype(F32)
+    stepped(g, *refs[2 * pairs + 2 : 2 * pairs + 5], *refs[-3:])
+
+
 def adamw_kernel(terms, steps, s, *refs):
     w, m, v = refs[2 * terms : 2 * terms + 3] if steps else refs[terms : terms + 3]
     new_w, new_m, new_v = refs[-3:]
 
     def block(gs):
-        g = gs[0][...].astype(F32)
-        if terms == 2:
-            g = (g + gs[1][...].astype(F32)).astype(BF16).astype(F32)
-        stepped(g, w, m, v, new_w, new_m, new_v)
+        @pl.loop(0, gs[0].shape[0], step=32)
+        def _(r):
+            rows = pl.ds(r, 32)
+            g = gs[0][rows].astype(F32)
+            if terms == 2:
+                g = (g + gs[1][rows].astype(F32)).astype(BF16).astype(F32)
+            stepped(g, w, m, v, new_w, new_m, new_v, rows)
 
     if steps:
         pl.when(pl.program_id(0) < steps)(lambda: block(refs[:terms]))
@@ -283,7 +309,7 @@
         far_h1, far_by1 = barrier((far_h1, far_by1, sums[GATE]))[:2]
         far_a1, far_hidden1, far_by_gate1, far_by_up1 = barrier(turn(far_h1, far_by1, w, 1, base[None].astype(jnp.int32), share))
 
-        def left1(side, which, got=None, behind=None):
+        def left1(side, which, got=None, behind=None, piece=None):
             if which == DOWN:
                 pairs = [(hidden1, by1), (far_hidden1, far_by1)]
                 places, size, n, tile = (chip * 2 + side, side, 0, 0), share // 2, d, TILE
@@ -292,21 +318,27 @@
                 places, size, n, tile = (side, side, base, 0), d // 2, share, TILE
             if behind is not None:
                 pairs[0] = (after(pairs[0][0], behind), pairs[0][1])
+            if piece is not None:
+                here = after(far[DOWN][piece], behind)
+                passed[piece] = partner(here)
+                terms = (sums[DOWN][piece], here)
+                total, *new[DOWN] = barrier(term((*places, me * 2 + piece), pairs, size, n, tile, so_far=new[DOWN], beside=(terms, old[DOWN], 0)))
+                return total
             if got is None:
                 return barrier(term(places, pairs, size, n, tile))
             corner = (chip * 2 + side, 0) if which == DOWN else (side, base)
-            total, *new[which] = barrier(term(places + corner, pairs, size, n, tile, got, old[which], 1))
+            total, *new[which] = barrier(term(places + corner, pairs, size, n, tile, got, old[which], 1, new[which]))
             return total
 
-        new, theirs, own1 = [None] * 3, {}, {}
+        new, theirs, own1, passed = [None] * 3, {}, {}, {}
         theirs[DOWN] = left1(sides[0], DOWN)
         got = partner(theirs[DOWN])
-        theirs[UP] = left1(sides[0], UP, None, theirs[DOWN])
+        theirs[UP] = left1(sides[0], UP, None, theirs[DOWN], 0)
         got_up = partner(theirs[UP])
         own1[DOWN] = left1(sides[1], DOWN, got, theirs[UP])
         far1 = {DOWN: across(own1[DOWN])}
         near1 = {DOWN: partner(own1[DOWN])}
-        theirs[GATE] = left1(sides[0], GATE, None, own1[DOWN])
+        theirs[GATE] = left1(sides[0], GATE, None, own1[DOWN], 1)
         got_gate = partner(theirs[GATE])
         own1[UP] = left1(sides[1], UP, got_up, theirs[GATE])
         far1[UP] = across(own1[UP])
@@ -332,11 +364,8 @@
 
         def first_layer(which):
             if which == DOWN:
-                here = list(barrier((*far[which], last))[:2])
                 places = [(side * 2, 0, side * 2 + 1, 0) for side in (me, 1 - me)]
-                optimize(which, 0, (sums[which][0], here[0]), places[0], 224, (sums[which][1], here[1]))
-                there = [partner(here[n]) for n in range(2)]
-                optimize(which, 0, (near[which][0], there[0]), places[1], 224, (near[which][1], there[1]))
+                optimize(which, 0, (near[which][0], passed[0]), places[1], 224, (near[which][1], passed[1]))
                 return
             here = after(far[which], last)
             optimize(which, 0, (sums[which], here), (me, 0), 192)

time: 1360 us -> 1270 us (0.934)
  waiting for transfers between devices: 500 us -> 408 us
    ppermute x9, waiting for transfers between devices: 497 us -> 408 us  [across(): return lax.ppermute(x, 'dp', ACROSS)]
    pallas_call x31 -> x30, Pallas kernels: 721 us -> 720 us  [call(): pl.pallas_call(kernel, grid_spec=pltpu.PrefetchScalarGridSpec(num_scalar_...]
  transfers between devices with their start and end apart: 30 -> 30, of which waited for: 10 -> 8; matrix products, arithmetic and copies ran while one was open for 1% -> 1% of each run, Pallas kernels for 31% -> 38%
where the time goes in v3:
time: 1270 us; the launch traced here: 1260 us
  Pallas kernels  720 us (57%)
  waiting for transfers between devices  408 us (32%)
  matrix products  92.3 us (7%)
  starting transfers between devices  18.2 us (1%)
  other arithmetic  16.6 us (1%)
    pallas_call x30, Pallas kernels, call(): pl.pallas_call(kernel, grid_spec=pltpu.PrefetchScalarGridSpec(num_scalar_...  720 us
    ppermute x9, waiting for transfers between devices, across(): return lax.ppermute(x, 'dp', ACROSS)  408 us
    dot_general x3, matrix products, dot(): return lax.dot_general(a, b, (dims, ((), ())), preferred_element_type=F32)  92.3 us
  transfers between devices with their start and end apart: 30, of which 8 were waited for; matrix products, arithmetic and copies ran while one was open for 1% of the time, Pallas kernels for 38%

profile of v3, /device:TPU:0, one launch (start us, length us, event | category | flops | bytes accessed | tf_op | source)
XLA Modules:
  0.0 1258.2 jit_solution(17614444528459471439)
XLA Ops:
  0.7 57.6 %shard_map.178 = (bf16[2048,1536]{1,0:T(8,128)(2,1)}, bf16[2048,3584]{1,0:T(8,128)(2,1)}, f32[2048,3584]{1,0:T(8,128)}, f32[2048,3584]{1,0:T(8,128)}) custom-call(s32[1]{0:T(128)} %constant.38.clone.1._, bf16[2048,1536]{1,0:T(8,128)(2,1)} %bitcast.45, bf16[2,1536,3584]{2,1,0:T(8,128)(2,1)} %refs_1_.9, bf16[2,1536,3584]{2,1,0:T(8,128)(2,1)} %refs_2_.19), custom_call_target="tpu_custom_call" | custom-call | flops 45097156608 | bytes 79691776 | tf_op jit(solution)/shard_map/pallas_call | solution.py:75
  58.2 30.3 %fusion.24.h = bf16[2048,1536]{1,0:T(8,128)(2,1)} fusion(bf16[2048,3584]{1,0:T(8,128)(2,1)} %get-tuple-element.129.refs_0_, bf16[2,3584,1536]{2,1,0:T(8,128)(2,1)} %refs_2_.18, bf16[1,2048,1536]{2,1,0:T(8,128)(2,1)} %param.11), kind=kOutput, calls=%fused_computation.21 | convolution fusion | flops 22554869760 | bytes 38273024 | tf_op jit(solution)/shard_map/dot_general | solution.py:22
  88.5 83.9 %shard_map.179 = (bf16[2048,1536]{1,0:T(8,128)(2,1)}, bf16[2048,3584]{1,0:T(8,128)(2,1)}, bf16[2048,3584]{1,0:T(8,128)(2,1)}, bf16[2048,3584]{1,0:T(8,128)(2,1)}) custom-call(s32[1]{0:T(128)} %constant.38.clone.1._, bf16[2048,1536]{1,0:T(8,128)(2,1)} %fusion.24.h, bf16[2048,1536]{1,0:T(8,128)(2,1)} %bitcast.41, bf16[2,1536,3584]{2,1,0:T(8,128)(2,1)} %refs_1_.9, ...), custom_call_target="tpu_custom_call" | custom-call | flops 67645734912 | bytes 50331648 | tf_op jit(solution)/shard_map/pallas_call | solution.py:75
  172.4 30.1 %fusion.16 = bf16[2048,1536]{1,0:T(8,128)(2,1)} fusion(bf16[2048,3584]{1,0:T(8,128)(2,1)} %get-tuple-element.125.refs_1_, bf16[2,1536,3584]{2,1,0:T(8,128)(2,1)} %refs_1_.9), kind=kOutput, calls=%fused_computation.19 | convolution fusion | flops 22551724032 | bytes 31981568 | tf_op jit(solution)/shard_map/dot_general | solution.py:22
  202.5 32.0 %fusion.2 = (f32[2048]{0:T(1024)S(1)}, f32[2048]{0:T(1024)S(1)}, bf16[2048,1536]{1,0:T(8,128)(2,1)}) fusion(bf16[2048,1536]{1,0:T(8,128)(2,1)} %fusion.24.h, bf16[2048,3584]{1,0:T(8,128)(2,1)} %get-tuple-element.126.refs_1_, bf16[2,1536,3584]{2,1,0:T(8,128)(2,1)} %refs_2_.19, bf16[2048,1536]{1,0:T(8,128)(2,1)} %fusion.16), kind=kOutput, calls=%fused_computation.6 | convolution fusion | flops 22583177216 | bytes 44580864 | tf_op jit(solution)/shard_map/dot_general | solution.py:22
  234.4 10.9 fusion.27.refs_1_.by
  245.3 0.6 pad_add_fusion
  246.0 11.5 shard_map.180
  257.4 0.8 collective-permute-start.2
  258.3 0.6 pad_add_fusion.2._
  258.9 11.4 shard_map.181
  270.3 0.6 pad_add_fusion.3._
  271.0 0.6 pad_add_fusion.4._
  271.6 0.7 pad_add_fusion.5
  272.3 12.1 shard_map.182.refs_4_
  284.4 11.9 shard_map.183.refs_4_
  296.3 44.9 %shard_map.184 = (bf16[2048,3584]{1,0:T(8,128)(2,1)}, bf16[2048,3584]{1,0:T(8,128)(2,1)}) custom-call(s32[1]{0:T(128)} %constant.38.clone.1._, bf16[2048,1536]{1,0:T(8,128)(2,1)} %fusion.27.refs_1_.by, bf16[2,3584,1536]{2,1,0:T(8,128)(2,1)} %refs_2_.18, f32[2048,3584]{1,0:T(8,128)} %get-tuple-element.131.gate, f32[2048,3584]{1,0:T(8,128)} %get-tuple-element.132.up), custom_call_target="tpu_custom_call" | custom-call | flops 22548578304 | bytes 29360128 | tf_op jit(solution)/shard_map/pallas_call | solution.py:75
  341.3 17.1 %shard_map.185 = bf16[768,3584]{1,0:T(8,128)(2,1)} custom-call(s32[2]{0:T(128)} %get-tuple-element.240._.s, bf16[2048,1536]{1,0:T(8,128)(2,1)} %get-tuple-element.137.refs_0_, bf16[2048,3584]{1,0:T(8,128)(2,1)} %get-tuple-element.133.refs_1_), custom_call_target="tpu_custom_call" | custom-call | flops 11274289152 | bytes 5505024 | tf_op jit(solution)/shard_map/pallas_call | solution.py:75
  358.3 0.5 collective-permute-start.4
  358.8 17.1 %shard_map.186 = bf16[768,3584]{1,0:T(8,128)(2,1)} custom-call(s32[2]{0:T(128)} %get-tuple-element.240._.s, bf16[2048,1536]{1,0:T(8,128)(2,1)} %get-tuple-element.137.refs_0_, bf16[2048,3584]{1,0:T(8,128)(2,1)} %get-tuple-element.135.refs_1_), custom_call_target="tpu_custom_call" | custom-call | flops 11274289152 | bytes 5505024 | tf_op jit(solution)/shard_map/pallas_call | solution.py:75
  375.9 3.0 collective-permute-start
  378.9 0.6 pad_add_fusion.6._.s
  379.5 0.7 pad_add_fusion.11
  380.1 2.0 collective-permute-start.6
  382.1 18.0 %shard_map.187.refs_0_ = bf16[768,3584]{1,0:T(8,128)(2,1)} custom-call(s32[2]{0:T(128)} %pad_add_fusion.6._.s, bf16[2048,1536]{1,0:T(8,128)(2,1)} %get-tuple-element.137.refs_0_, bf16[2048,3584]{1,0:T(8,128)(2,1)} %get-tuple-element.133.refs_1_, bf16[768,3584]{1,0:T(8,128)(2,1)} %collective-permute-done.4.refs_2_), custom_call_target="tpu_custom_call" | custom-call | flops 11274289152 | bytes 5505024 | tf_op jit(solution)/shard_map/pallas_call | solution.py:75
  400.1 18.0 %shard_map.188.refs_0_ = bf16[768,3584]{1,0:T(8,128)(2,1)} custom-call(s32[2]{0:T(128)} %pad_add_fusion.6._.s, bf16[2048,1536]{1,0:T(8,128)(2,1)} %get-tuple-element.137.refs_0_, bf16[2048,3584]{1,0:T(8,128)(2,1)} %get-tuple-element.135.refs_1_, bf16[768,3584]{1,0:T(8,128)(2,1)} %collective-permute-done.5.refs_2_), custom_call_target="tpu_custom_call" | custom-call | flops 11274289152 | bytes 5505024 | tf_op jit(solution)/shard_map/pallas_call | solution.py:75
  418.1 97.5 %collective-permute-done.h = bf16[2048,1536]{1,0:T(8,128)(2,1)} collective-permute-done((bf16[2048,1536]{1,0:T(8,128)(2,1)}, bf16[2048,1536]{1,0:T(8,128)(2,1)}, u32[]{:S(2)}, u32[]{:S(2)}) %collective-permute-start) | collective-permute-done | bytes 6291488 | tf_op jit(solution)/shard_map/ppermute | solution.py:264
  515.6 134.8 %collective-permute-done.1.by.refs_3_ = bf16[2048,1536]{1,0:T(8,128)(2,1)} collective-permute-done((bf16[2048,1536]{1,0:T(8,128)(2,1)}, bf16[2048,1536]{1,0:T(8,128)(2,1)}, u32[]{:S(2)}, u32[]{:S(2)}) %collective-permute-start.1) | collective-permute-done | bytes 6291488 | tf_op jit(solution)/shard_map/ppermute | solution.py:264
  650.4 47.7 %shard_map.189 = (bf16[2048,1536]{1,0:T(8,128)(2,1)}, bf16[2048,1792]{1,0:T(8,128)(2,1)}, bf16[2048,1792]{1,0:T(8,128)(2,1)}, bf16[2048,1792]{1,0:T(8,128)(2,1)}) custom-call(s32[1]{0:T(128)} %bitcast.3._, bf16[2048,1536]{1,0:T(8,128)(2,1)} %collective-permute-done.h, bf16[2048,1536]{1,0:T(8,128)(2,1)} %collective-permute-done.1.by.refs_3_, ...), custom_call_target="tpu_custom_call" | custom-call | flops 33822867456 | bytes 28311552 | tf_op jit(solution)/shard_map/pallas_call | solution.py:75
  698.1 18.1 %shard_map.190 = bf16[896,1536]{1,0:T(8,128)(2,1)} custom-call(s32[4]{0:T(128)} %get-tuple-element.242._, bf16[2048,3584]{1,0:T(8,128)(2,1)} %get-tuple-element.146.refs_0_, bf16[2048,1536]{1,0:T(8,128)(2,1)} %bitcast.43, bf16[2048,1792]{1,0:T(8,128)(2,1)} %get-tuple-element.140.refs_2_, bf16[2048,1536]{1,0:T(8,128)(2,1)} %collective-permute-done.1.by.refs_3_), custom_call_target="tpu_custom_call" | custom-call | flops 11274289152 | bytes 2752512 | tf_op jit(solution)/shard_map/pallas_call | solution.py:75
  716.2 2.0 collective-permute-start.8
  718.2 0.6 stack.73._
  718.8 0.6 stack.69._
  719.4 0.6 stack.71._
  720.5 27.4 %shard_map.191 = (bf16[768,1792]{1,0:T(8,128)(2,1)}, bf16[2,3584,1536]{2,1,0:T(8,128)(2,1)}, f32[2,3584,1536]{2,1,0:T(8,128)}, f32[2,3584,1536]{2,1,0:T(8,128)}) custom-call(s32[5]{0:T(128)} %stack.73._, bf16[2048,1536]{1,0:T(8,128)(2,1)} %get-tuple-element.160.refs_0_, bf16[2048,3584]{1,0:T(8,128)(2,1)} %get-tuple-element.126.refs_1_, ...), custom_call_target="tpu_custom_call" | custom-call | flops 11274289152 | bytes 112852992 | tf_op jit(solution)/shard_map/pallas_call | solution.py:75
  748.2 24.7 %shard_map.192 = (bf16[896,1536]{1,0:T(8,128)(2,1)}, bf16[2,3584,1536]{2,1,0:T(8,128)(2,1)}, f32[2,3584,1536]{2,1,0:T(8,128)}, f32[2,3584,1536]{2,1,0:T(8,128)}) custom-call(s32[6]{0:T(128)} %stack.71._, bf16[2048,3584]{1,0:T(8,128)(2,1)} %get-tuple-element.146.refs_0_, ...), custom_call_target="tpu_custom_call", output_to_operand_aliasing={{1}: (9, {}), {2}: (10, {}), {3}: (11, {})} | custom-call | flops 11274289152 | bytes 112852992 | tf_op jit(solution)/shard_map/pallas_call | solution.py:75
  772.9 6.0 collective-permute-done.8.refs_5_
  778.9 27.6 %shard_map.193 = (bf16[768,1792]{1,0:T(8,128)(2,1)}, bf16[2,3584,1536]{2,1,0:T(8,128)(2,1)}, f32[2,3584,1536]{2,1,0:T(8,128)}, f32[2,3584,1536]{2,1,0:T(8,128)}) custom-call(s32[5]{0:T(128)} %stack.69._, bf16[2048,1536]{1,0:T(8,128)(2,1)} %get-tuple-element.160.refs_0_, ...), custom_call_target="tpu_custom_call", output_to_operand_aliasing={{1}: (10, {}), {2}: (11, {}), {3}: (12, {})} | custom-call | flops 11274289152 | bytes 112852992 | tf_op jit(solution)/shard_map/pallas_call | solution.py:75
  807.0 1.7 collective-permute-start.16
  808.7 0.7 stack.67._
  809.4 25.1 %shard_map.194 = (bf16[768,1792]{1,0:T(8,128)(2,1)}, bf16[2,1536,3584]{2,1,0:T(8,128)(2,1)}, f32[2,1536,3584]{2,1,0:T(8,128)}, f32[2,1536,3584]{2,1,0:T(8,128)}) custom-call(s32[6]{0:T(128)} %stack.67._, bf16[2048,1536]{1,0:T(8,128)(2,1)} %get-tuple-element.160.refs_0_, bf16[2048,3584]{1,0:T(8,128)(2,1)} %get-tuple-element.126.refs_1_, ...), custom_call_target="tpu_custom_call" | custom-call | flops 11274289152 | bytes 112852992 | tf_op jit(solution)/shard_map/pallas_call | solution.py:75
  835.1 25.0 %shard_map.195 = (bf16[768,1792]{1,0:T(8,128)(2,1)}, bf16[2,1536,3584]{2,1,0:T(8,128)(2,1)}, f32[2,1536,3584]{2,1,0:T(8,128)}, f32[2,1536,3584]{2,1,0:T(8,128)}) custom-call(s32[6]{0:T(128)} %stack.67._, bf16[2048,1536]{1,0:T(8,128)(2,1)} %get-tuple-element.160.refs_0_, bf16[2048,3584]{1,0:T(8,128)(2,1)} %get-tuple-element.125.refs_1_, ...), custom_call_target="tpu_custom_call" | custom-call | flops 11274289152 | bytes 112852992 | tf_op jit(solution)/shard_map/pallas_call | solution.py:75
  860.4 0.6 pad_add_fusion.7
  861.2 24.7 %shard_map.196 = (bf16[2,3584,1536]{2,1,0:T(8,128)(2,1)}, f32[2,3584,1536]{2,1,0:T(8,128)}, f32[2,3584,1536]{2,1,0:T(8,128)}) custom-call(s32[4]{0:T(128)} %get-tuple-element.247.s, bf16[896,1536]{1,0:T(8,128)(2,1)} %collective-permute-done.20.refs_0_, ...), custom_call_target="tpu_custom_call", output_to_operand_aliasing={{0}: (8, {}), {1}: (9, {}), {2}: (10, {})} | custom-call | flops 5505024000 | bytes 110100480 | tf_op jit(solution)/shard_map/pallas_call | solution.py:75
  886.0 12.1 shard_map.197
  898.1 12.1 shard_map.198
  910.2 12.1 shard_map.199
  922.4 5.5 collective-permute-done.16.refs_1_
  927.9 1.7 collective-permute-start.14
  929.9 22.3 %shard_map.200 = (bf16[2,1536,3584]{2,1,0:T(8,128)(2,1)}, f32[2,1536,3584]{2,1,0:T(8,128)}, f32[2,1536,3584]{2,1,0:T(8,128)}) custom-call(s32[2]{0:T(128)} %pad_add_fusion.6._.s, bf16[768,3584]{1,0:T(8,128)(2,1)} %shard_map.187.refs_0_, ...), custom_call_target="tpu_custom_call", output_to_operand_aliasing={{0}: (6, {}), {1}: (7, {}), {2}: (8, {})} | custom-call | flops 11010048000 | bytes 110100480 | tf_op jit(solution)/shard_map/pallas_call | solution.py:75
  952.2 22.3 %shard_map.201 = (bf16[2,1536,3584]{2,1,0:T(8,128)(2,1)}, f32[2,1536,3584]{2,1,0:T(8,128)}, f32[2,1536,3584]{2,1,0:T(8,128)}) custom-call(s32[2]{0:T(128)} %get-tuple-element.240._.s, bf16[768,3584]{1,0:T(8,128)(2,1)} %collective-permute-done.15.refs_0_, ...), custom_call_target="tpu_custom_call", output_to_operand_aliasing={{0}: (6, {}), {1}: (7, {}), {2}: (8, {})} | custom-call | flops 11010048000 | bytes 110100480 | tf_op jit(solution)/shard_map/pallas_call | solution.py:75
  974.5 74.8 %collective-permute-done.14.refs_1_ = bf16[768,3584]{1,0:T(8,128)(2,1)} collective-permute-done((bf16[768,3584]{1,0:T(8,128)(2,1)}, bf16[768,3584]{1,0:T(8,128)(2,1)}, u32[]{:S(2)}, u32[]{:S(2)}) %collective-permute-start.14) | collective-permute-done | bytes 5505056 | tf_op jit(solution)/shard_map/ppermute | solution.py:264
  1049.3 1.7 collective-permute-start.27
  1051.3 22.5 %shard_map.202 = (bf16[2,1536,3584]{2,1,0:T(8,128)(2,1)}, f32[2,1536,3584]{2,1,0:T(8,128)}, f32[2,1536,3584]{2,1,0:T(8,128)}) custom-call(s32[2]{0:T(128)} %pad_add_fusion.6._.s, bf16[768,3584]{1,0:T(8,128)(2,1)} %shard_map.188.refs_0_, ...), custom_call_target="tpu_custom_call", output_to_operand_aliasing={{0}: (6, {}), {1}: (7, {}), {2}: (8, {})} | custom-call | flops 11010048000 | bytes 110100480 | tf_op jit(solution)/shard_map/pallas_call | solution.py:75
  1073.8 38.3 %collective-permute-done.27.refs_0_ = bf16[896,1536]{1,0:T(8,128)(2,1)} collective-permute-done((bf16[896,1536]{1,0:T(8,128)(2,1)}, bf16[896,1536]{1,0:T(8,128)(2,1)}, u32[]{:S(2)}, u32[]{:S(2)}) %collective-permute-start.27) | collective-permute-done | bytes 2752544 | tf_op jit(solution)/shard_map/ppermute | solution.py:264
  1112.2 22.4 %shard_map.203 = (bf16[2,1536,3584]{2,1,0:T(8,128)(2,1)}, f32[2,1536,3584]{2,1,0:T(8,128)}, f32[2,1536,3584]{2,1,0:T(8,128)}) custom-call(s32[2]{0:T(128)} %get-tuple-element.240._.s, bf16[768,3584]{1,0:T(8,128)(2,1)} %collective-permute-done.13.refs_0_, ...), custom_call_target="tpu_custom_call", output_to_operand_aliasing={{0}: (6, {}), {1}: (7, {}), {2}: (8, {})} | custom-call | flops 11010048000 | bytes 110100480 | tf_op jit(solution)/shard_map/pallas_call | solution.py:75
  1134.6 36.1 %collective-permute-done.12.refs_0_ = bf16[768,1792]{1,0:T(8,128)(2,1)} collective-permute-done((bf16[768,1792]{1,0:T(8,128)(2,1)}, bf16[768,1792]{1,0:T(8,128)(2,1)}, u32[]{:S(2)}, u32[]{:S(2)}) %collective-permute-start.12) | collective-permute-done | bytes 2752544 | tf_op jit(solution)/shard_map/ppermute | solution.py:264
  1170.7 1.7 collective-permute-start.11
  1172.4 23.1 %shard_map.204 = (bf16[2,3584,1536]{2,1,0:T(8,128)(2,1)}, f32[2,3584,1536]{2,1,0:T(8,128)}, f32[2,3584,1536]{2,1,0:T(8,128)}) custom-call(s32[4]{0:T(128)} %get-tuple-element.246.s, bf16[896,1536]{1,0:T(8,128)(2,1)} %collective-permute-done.27.refs_0_, ...), custom_call_target="tpu_custom_call", output_to_operand_aliasing={{0}: (6, {}), {1}: (7, {}), {2}: (8, {})} | custom-call | flops 5505024000 | bytes 110100480 | tf_op jit(solution)/shard_map/pallas_call | solution.py:75
  1195.6 23.1 %shard_map.205 = (bf16[2,1536,3584]{2,1,0:T(8,128)(2,1)}, f32[2,1536,3584]{2,1,0:T(8,128)}, f32[2,1536,3584]{2,1,0:T(8,128)}) custom-call(s32[4]{0:T(128)} %get-tuple-element.243.s, bf16[768,1792]{1,0:T(8,128)(2,1)} %collective-permute-done.12.refs_0_, ...), custom_call_target="tpu_custom_call", output_to_operand_aliasing={{0}: (6, {}), {1}: (7, {}), {2}: (8, {})} | custom-call | flops 5505024000 | bytes 110100480 | tf_op jit(solution)/shard_map/pallas_call | solution.py:75
  1218.6 14.5 %collective-permute-done.11.refs_0_ = bf16[768,1792]{1,0:T(8,128)(2,1)} collective-permute-done((bf16[768,1792]{1,0:T(8,128)(2,1)}, bf16[768,1792]{1,0:T(8,128)(2,1)}, u32[]{:S(2)}, u32[]{:S(2)}) %collective-permute-start.11) | collective-permute-done | bytes 2752544 | tf_op jit(solution)/shard_map/ppermute | solution.py:264
  1233.1 0.7 pad_add_fusion.14
  1233.8 12.1 shard_map.206
  1245.9 12.1 shard_map.207
  (45 shorter events, 3.0 us)
Async XLA Ops:
  257.4 14.8 %collective-permute-start.2 = (bf16[896,1536]{1,0:T(8,128)(2,1)}, bf16[896,1536]{1,0:T(8,128)(2,1)}, u32[]{:S(2)}, u32[]{:S(2)}) collective-permute-start(bf16[896,1536]{1,0:T(8,128)(2,1)} %shard_map.180), channel_id=1, source_target_pairs={{0,1},{1,0},{2,3},{3,2},{4,5},{5,4},{6,7},{7,6}} | collective-permute-start | bytes 8257544 | tf_op jit(solution)/shard_map/ppermute | solution.py:267
  270.3 14.1 %collective-permute-start.3 = (bf16[896,1536]{1,0:T(8,128)(2,1)}, bf16[896,1536]{1,0:T(8,128)(2,1)}, u32[]{:S(2)}, u32[]{:S(2)}) collective-permute-start(bf16[896,1536]{1,0:T(8,128)(2,1)} %shard_map.181), channel_id=1, source_target_pairs={{0,1},{1,0},{2,3},{3,2},{4,5},{5,4},{6,7},{7,6}} | collective-permute-start | bytes 8257544 | tf_op jit(solution)/shard_map/ppermute | solution.py:267
  358.3 23.8 %collective-permute-start.4 = (bf16[768,3584]{1,0:T(8,128)(2,1)}, bf16[768,3584]{1,0:T(8,128)(2,1)}, u32[]{:S(2)}, u32[]{:S(2)}) collective-permute-start(bf16[768,3584]{1,0:T(8,128)(2,1)} %shard_map.185), channel_id=1, source_target_pairs={{0,1},{1,0},{2,3},{3,2},{4,5},{5,4},{6,7},{7,6}} | collective-permute-start | bytes 16515080 | tf_op jit(solution)/shard_map/ppermute | solution.py:267
  375.9 24.2 %collective-permute-start.5 = (bf16[768,3584]{1,0:T(8,128)(2,1)}, bf16[768,3584]{1,0:T(8,128)(2,1)}, u32[]{:S(2)}, u32[]{:S(2)}) collective-permute-start(bf16[768,3584]{1,0:T(8,128)(2,1)} %shard_map.186), channel_id=1, source_target_pairs={{0,1},{1,0},{2,3},{3,2},{4,5},{5,4},{6,7},{7,6}} | collective-permute-start | bytes 16515080 | tf_op jit(solution)/shard_map/ppermute | solution.py:267
  375.9 139.7 %collective-permute-start = (bf16[2048,1536]{1,0:T(8,128)(2,1)}, bf16[2048,1536]{1,0:T(8,128)(2,1)}, u32[]{:S(2)}, u32[]{:S(2)}) collective-permute-start(bf16[2048,1536]{1,0:T(8,128)(2,1)} %fusion.24.h), channel_id=1, source_target_pairs={{0,2},{2,0},{1,3},{3,1},{4,6},{6,4},{5,7},{7,5}} | collective-permute-start | bytes 18874376 | tf_op jit(solution)/shard_map/ppermute | solution.py:264
  378.9 271.5 %collective-permute-start.1 = (bf16[2048,1536]{1,0:T(8,128)(2,1)}, bf16[2048,1536]{1,0:T(8,128)(2,1)}, u32[]{:S(2)}, u32[]{:S(2)}) collective-permute-start(bf16[2048,1536]{1,0:T(8,128)(2,1)} %bitcast.42), channel_id=1, source_target_pairs={{0,2},{2,0},{1,3},{3,1},{4,6},{6,4},{5,7},{7,5}} | collective-permute-start | bytes 18874376 | tf_op jit(solution)/shard_map/ppermute | solution.py:264
  380.1 340.4 %collective-permute-start.6 = (bf16[896,1536]{1,0:T(8,128)(2,1)}, bf16[896,1536]{1,0:T(8,128)(2,1)}, u32[]{:S(2)}, u32[]{:S(2)}) collective-permute-start(bf16[896,1536]{1,0:T(8,128)(2,1)} %shard_map.182.refs_4_), channel_id=1, source_target_pairs={{0,2},{2,0},{1,3},{3,1},{4,6},{6,4},{5,7},{7,5}} | collective-permute-start | bytes 8257544 | tf_op jit(solution)/shard_map/ppermute | solution.py:264
  716.2 32.0 %collective-permute-start.7 = (bf16[896,1536]{1,0:T(8,128)(2,1)}, bf16[896,1536]{1,0:T(8,128)(2,1)}, u32[]{:S(2)}, u32[]{:S(2)}) collective-permute-start(bf16[896,1536]{1,0:T(8,128)(2,1)} %shard_map.190), channel_id=1, source_target_pairs={{0,1},{1,0},{2,3},{3,2},{4,5},{5,4},{6,7},{7,6}} | collective-permute-start | bytes 8257544 | tf_op jit(solution)/shard_map/ppermute | solution.py:267
  716.2 62.7 %collective-permute-start.8 = (bf16[896,1536]{1,0:T(8,128)(2,1)}, bf16[896,1536]{1,0:T(8,128)(2,1)}, u32[]{:S(2)}, u32[]{:S(2)}) collective-permute-start(bf16[896,1536]{1,0:T(8,128)(2,1)} %shard_map.183.refs_4_), channel_id=1, source_target_pairs={{0,2},{2,0},{1,3},{3,1},{4,6},{6,4},{5,7},{7,5}} | collective-permute-start | bytes 8257544 | tf_op jit(solution)/shard_map/ppermute | solution.py:264
  720.0 87.0 %collective-permute-start.22 = (bf16[896,1536]{1,0:T(8,128)(2,1)}, bf16[896,1536]{1,0:T(8,128)(2,1)}, u32[]{:S(2)}, u32[]{:S(2)}) collective-permute-start(bf16[896,1536]{1,0:T(8,128)(2,1)} %shard_map.183.refs_4_), channel_id=1, source_target_pairs={{0,1},{1,0},{2,3},{3,2},{4,5},{5,4},{6,7},{7,6}} | collective-permute-start | bytes 8257544 | tf_op jit(solution)/shard_map/ppermute | solution.py:267
  720.3 114.3 %collective-permute-start.20 = (bf16[896,1536]{1,0:T(8,128)(2,1)}, bf16[896,1536]{1,0:T(8,128)(2,1)}, u32[]{:S(2)}, u32[]{:S(2)}) collective-permute-start(bf16[896,1536]{1,0:T(8,128)(2,1)} %shard_map.182.refs_4_), channel_id=1, source_target_pairs={{0,1},{1,0},{2,3},{3,2},{4,5},{5,4},{6,7},{7,6}} | collective-permute-start | bytes 8257544 | tf_op jit(solution)/shard_map/ppermute | solution.py:267
  747.9 61.5 %collective-permute-start.9 = (bf16[768,1792]{1,0:T(8,128)(2,1)}, bf16[768,1792]{1,0:T(8,128)(2,1)}, u32[]{:S(2)}, u32[]{:S(2)}) collective-permute-start(bf16[768,1792]{1,0:T(8,128)(2,1)} %get-tuple-element.145), channel_id=1, source_target_pairs={{0,1},{1,0},{2,3},{3,2},{4,5},{5,4},{6,7},{7,6}} | collective-permute-start | bytes 8257544 | tf_op jit(solution)/shard_map/ppermute | solution.py:267
  806.5 28.5 %collective-permute-start.10 = (bf16[768,1792]{1,0:T(8,128)(2,1)}, bf16[768,1792]{1,0:T(8,128)(2,1)}, u32[]{:S(2)}, u32[]{:S(2)}) collective-permute-start(bf16[768,1792]{1,0:T(8,128)(2,1)} %get-tuple-element.157), channel_id=1, source_target_pairs={{0,1},{1,0},{2,3},{3,2},{4,5},{5,4},{6,7},{7,6}} | collective-permute-start | bytes 8257544 | tf_op jit(solution)/shard_map/ppermute | solution.py:267
  806.5 53.6 %collective-permute-start.21 = (bf16[896,1536]{1,0:T(8,128)(2,1)}, bf16[896,1536]{1,0:T(8,128)(2,1)}, u32[]{:S(2)}, u32[]{:S(2)}) collective-permute-start(bf16[896,1536]{1,0:T(8,128)(2,1)} %collective-permute-done.6.refs_5_), channel_id=1, source_target_pairs={{0,1},{1,0},{2,3},{3,2},{4,5},{5,4},{6,7},{7,6}} | collective-permute-start | bytes 8257544 | tf_op jit(solution)/shard_map/ppermute | solution.py:267
  807.0 120.9 %collective-permute-start.16 = (bf16[768,3584]{1,0:T(8,128)(2,1)}, bf16[768,3584]{1,0:T(8,128)(2,1)}, u32[]{:S(2)}, u32[]{:S(2)}) collective-permute-start(bf16[768,3584]{1,0:T(8,128)(2,1)} %shard_map.187.refs_0_), channel_id=1, source_target_pairs={{0,2},{2,0},{1,3},{3,1},{4,6},{6,4},{5,7},{7,5}} | collective-permute-start | bytes 16515080 | tf_op jit(solution)/shard_map/ppermute | solution.py:264
  809.4 51.6 %collective-permute-start.23 = (bf16[896,1536]{1,0:T(8,128)(2,1)}, bf16[896,1536]{1,0:T(8,128)(2,1)}, u32[]{:S(2)}, u32[]{:S(2)}) collective-permute-start(bf16[896,1536]{1,0:T(8,128)(2,1)} %collective-permute-done.8.refs_5_), channel_id=1, source_target_pairs={{0,1},{1,0},{2,3},{3,2},{4,5},{5,4},{6,7},{7,6}} | collective-permute-start | bytes 8257544 | tf_op jit(solution)/shard_map/ppermute | solution.py:267
  834.5 51.4 %collective-permute-start.19 = (bf16[896,1536]{1,0:T(8,128)(2,1)}, bf16[896,1536]{1,0:T(8,128)(2,1)}, u32[]{:S(2)}, u32[]{:S(2)}) collective-permute-start(bf16[896,1536]{1,0:T(8,128)(2,1)} %get-tuple-element.150), channel_id=1, source_target_pairs={{0,1},{1,0},{2,3},{3,2},{4,5},{5,4},{6,7},{7,6}} | collective-permute-start | bytes 8257544 | tf_op jit(solution)/shard_map/ppermute | solution.py:267
  834.9 63.2 %collective-permute-start.18 = (bf16[768,1792]{1,0:T(8,128)(2,1)}, bf16[768,1792]{1,0:T(8,128)(2,1)}, u32[]{:S(2)}, u32[]{:S(2)}) collective-permute-start(bf16[768,1792]{1,0:T(8,128)(2,1)} %get-tuple-element.159), channel_id=1, source_target_pairs={{0,1},{1,0},{2,3},{3,2},{4,5},{5,4},{6,7},{7,6}} | collective-permute-start | bytes 8257544 | tf_op jit(solution)/shard_map/ppermute | solution.py:267
  860.1 50.1 %collective-permute-start.17 = (bf16[768,1792]{1,0:T(8,128)(2,1)}, bf16[768,1792]{1,0:T(8,128)(2,1)}, u32[]{:S(2)}, u32[]{:S(2)}) collective-permute-start(bf16[768,1792]{1,0:T(8,128)(2,1)} %get-tuple-element.161), channel_id=1, source_target_pairs={{0,1},{1,0},{2,3},{3,2},{4,5},{5,4},{6,7},{7,6}} | collective-permute-start | bytes 8257544 | tf_op jit(solution)/shard_map/ppermute | solution.py:267
  861.0 91.2 %collective-permute-start.15 = (bf16[768,3584]{1,0:T(8,128)(2,1)}, bf16[768,3584]{1,0:T(8,128)(2,1)}, u32[]{:S(2)}, u32[]{:S(2)}) collective-permute-start(bf16[768,3584]{1,0:T(8,128)(2,1)} %shard_map.187.refs_0_), channel_id=1, source_target_pairs={{0,1},{1,0},{2,3},{3,2},{4,5},{5,4},{6,7},{7,6}} | collective-permute-start | bytes 16515080 | tf_op jit(solution)/shard_map/ppermute | solution.py:267
  927.9 24.3 %collective-permute-start.24 = (bf16[768,3584]{1,0:T(8,128)(2,1)}, bf16[768,3584]{1,0:T(8,128)(2,1)}, u32[]{:S(2)}, u32[]{:S(2)}) collective-permute-start(bf16[768,3584]{1,0:T(8,128)(2,1)} %collective-permute-done.16.refs_1_), channel_id=1, source_target_pairs={{0,1},{1,0},{2,3},{3,2},{4,5},{5,4},{6,7},{7,6}} | collective-permute-start | bytes 16515080 | tf_op jit(solution)/shard_map/ppermute | solution.py:267
  927.9 121.4 %collective-permute-start.14 = (bf16[768,3584]{1,0:T(8,128)(2,1)}, bf16[768,3584]{1,0:T(8,128)(2,1)}, u32[]{:S(2)}, u32[]{:S(2)}) collective-permute-start(bf16[768,3584]{1,0:T(8,128)(2,1)} %shard_map.188.refs_0_), channel_id=1, source_target_pairs={{0,2},{2,0},{1,3},{3,1},{4,6},{6,4},{5,7},{7,5}} | collective-permute-start | bytes 16515080 | tf_op jit(solution)/shard_map/ppermute | solution.py:264
  929.7 182.5 %collective-permute-start.13 = (bf16[768,3584]{1,0:T(8,128)(2,1)}, bf16[768,3584]{1,0:T(8,128)(2,1)}, u32[]{:S(2)}, u32[]{:S(2)}) collective-permute-start(bf16[768,3584]{1,0:T(8,128)(2,1)} %shard_map.188.refs_0_), channel_id=1, source_target_pairs={{0,1},{1,0},{2,3},{3,2},{4,5},{5,4},{6,7},{7,6}} | collective-permute-start | bytes 16515080 | tf_op jit(solution)/shard_map/ppermute | solution.py:267
  1049.3 62.9 %collective-permute-start.25 = (bf16[768,3584]{1,0:T(8,128)(2,1)}, bf16[768,3584]{1,0:T(8,128)(2,1)}, u32[]{:S(2)}, u32[]{:S(2)}) collective-permute-start(bf16[768,3584]{1,0:T(8,128)(2,1)} %collective-permute-done.14.refs_1_), channel_id=1, source_target_pairs={{0,1},{1,0},{2,3},{3,2},{4,5},{5,4},{6,7},{7,6}} | collective-permute-start | bytes 16515080 | tf_op jit(solution)/shard_map/ppermute | solution.py:267
  1049.3 62.9 %collective-permute-start.27 = (bf16[896,1536]{1,0:T(8,128)(2,1)}, bf16[896,1536]{1,0:T(8,128)(2,1)}, u32[]{:S(2)}, u32[]{:S(2)}) collective-permute-start(bf16[896,1536]{1,0:T(8,128)(2,1)} %get-tuple-element.150), channel_id=1, source_target_pairs={{0,2},{2,0},{1,3},{3,1},{4,6},{6,4},{5,7},{7,5}} | collective-permute-start | bytes 8257544 | tf_op jit(solution)/shard_map/ppermute | solution.py:264
  1051.1 119.6 %collective-permute-start.12 = (bf16[768,1792]{1,0:T(8,128)(2,1)}, bf16[768,1792]{1,0:T(8,128)(2,1)}, u32[]{:S(2)}, u32[]{:S(2)}) collective-permute-start(bf16[768,1792]{1,0:T(8,128)(2,1)} %get-tuple-element.159), channel_id=1, source_target_pairs={{0,2},{2,0},{1,3},{3,1},{4,6},{6,4},{5,7},{7,5}} | collective-permute-start | bytes 8257544 | tf_op jit(solution)/shard_map/ppermute | solution.py:264
  1112.2 60.3 %collective-permute-start.28 = (bf16[896,1536]{1,0:T(8,128)(2,1)}, bf16[896,1536]{1,0:T(8,128)(2,1)}, u32[]{:S(2)}, u32[]{:S(2)}) collective-permute-start(bf16[896,1536]{1,0:T(8,128)(2,1)} %collective-permute-done.27.refs_0_), channel_id=1, source_target_pairs={{0,1},{1,0},{2,3},{3,2},{4,5},{5,4},{6,7},{7,6}} | collective-permute-start | bytes 8257544 | tf_op jit(solution)/shard_map/ppermute | solution.py:267
  1170.7 24.9 %collective-permute-start.26 = (bf16[768,1792]{1,0:T(8,128)(2,1)}, bf16[768,1792]{1,0:T(8,128)(2,1)}, u32[]{:S(2)}, u32[]{:S(2)}) collective-permute-start(bf16[768,1792]{1,0:T(8,128)(2,1)} %collective-permute-done.12.refs_0_), channel_id=1, source_target_pairs={{0,1},{1,0},{2,3},{3,2},{4,5},{5,4},{6,7},{7,6}} | collective-permute-start | bytes 8257544 | tf_op jit(solution)/shard_map/ppermute | solution.py:267
  1170.7 62.4 %collective-permute-start.11 = (bf16[768,1792]{1,0:T(8,128)(2,1)}, bf16[768,1792]{1,0:T(8,128)(2,1)}, u32[]{:S(2)}, u32[]{:S(2)}) collective-permute-start(bf16[768,1792]{1,0:T(8,128)(2,1)} %get-tuple-element.161), channel_id=1, source_target_pairs={{0,2},{2,0},{1,3},{3,1},{4,6},{6,4},{5,7},{7,5}} | collective-permute-start | bytes 8257544 | tf_op jit(solution)/shard_map/ppermute | solution.py:264
  1233.1 12.8 %collective-permute-start.29 = (bf16[768,1792]{1,0:T(8,128)(2,1)}, bf16[768,1792]{1,0:T(8,128)(2,1)}, u32[]{:S(2)}, u32[]{:S(2)}) collective-permute-start(bf16[768,1792]{1,0:T(8,128)(2,1)} %collective-permute-done.11.refs_0_), channel_id=1, source_target_pairs={{0,1},{1,0},{2,3},{3,2},{4,5},{5,4},{6,7},{7,6}} | collective-permute-start | bytes 8257544 | tf_op jit(solution)/shard_map/ppermute | solution.py:267
